TPU v7x, 256 devices: a whole 4x4x8 slice. The times are simulated.
256 devices in a mesh: batch: 4 (over z_hi), seq: 64 (over y, x, z_lo, core).
Axes of the slice: x: 4, y: 4, z: 8 (z_hi: 4, z_lo: 2; z = z_hi * 2 + z_lo), core: 2. Of those that a mesh axis runs over, the one named last changes fastest.
Arguments:
- tokens: bfloat16 [2, 64, 8192], P(None, 'batch', 'seq'), may hold values from -8 to 8
- norm_gain: bfloat16 [8192], P('seq'), may hold values from 0.5 to 1.5
- w_qkv: bfloat16 [8192, 10240], P('batch', 'seq'), may hold values from -0.0625 to 0.0625
- w_out: bfloat16 [8192, 8192], P('seq'), may hold values from -1.5 to 1.5
- cache_keys: bfloat16 [64, 8192, 1024], P('batch', 'seq'), may hold values from -120 to 120
- cache_values: bfloat16 [64, 8192, 1024], P('batch', 'seq'), may hold values from -6 to 6
- lengths: int32 [64], P('batch'), may hold values from 2048 to 8190
- positions: int32 [64], P('batch'), may hold values from 0 to 32767
Outputs:
- mixed: bfloat16 [2, 64, 8192], P(None, 'batch', 'seq')
Inputs may be any that keep to these rules, and one draw needn't show every extreme that they name: `lengths`: filled cache positions of a sequence; its two new tokens take the next two positions.
All inputs are finite; a program needn't handle non-finite values.
Results may differ from a plain program's by a relative error of at most 0.01255.
The roundings to bfloat16 on the way count: a program that leaves them out, or rounds other values in their place, can miss the bound.
Values may be sent and summed in bfloat16 or wider, within the bound.
A program may use at most 128 MiB of HBM per device.

v0:
```python
import math

import jax
import jax.numpy as jnp
from jax import lax
from jax.sharding import PartitionSpec as P

D = 8192
H = 64
KVH = 8
HD = 128


rope_base = 500000.0
epsilon = 1e-05
lowest = -1e30


def sent_to_all(array, axis):
    devices = lax.axis_size(axis)
    return lax.all_to_all(
        jnp.broadcast_to(array[None], (devices, *array.shape)), axis, 0, 0, tiled=True
    )


def of_everyone(array, axis):
    return sent_to_all(array, axis).sum(axis=0)


def in_order(pieces, dim):
    dims = list(pieces.shape[1:])
    dims[dim] *= pieces.shape[0]
    return jnp.moveaxis(pieces, 0, dim).reshape(dims)


def collect(array, axis, dim):
    return in_order(sent_to_all(array, axis), dim)


def split_up(array, dim, devices):
    dims = array.shape
    pieces = array.reshape(*dims[:dim], devices, dims[dim] // devices, *dims[dim + 1 :])
    return jnp.moveaxis(pieces, dim, 0)


def summed_on_arrival(array, axis, dim):
    devices = lax.axis_size(axis)
    pieces = lax.all_to_all(split_up(array, dim, devices), axis, 0, 0, tiled=True)
    return jnp.sum(pieces, axis=0)


def sent_together(arrays, axis, split_dim, concat_dim, along):
    columns = [a.reshape(*a.shape[:along], -1) for a in arrays]
    both = jnp.concatenate(columns, axis=along)
    out, at, outs = (
        lax.all_to_all(both, axis, split_axis=split_dim, concat_axis=concat_dim, tiled=True),
        0,
        [],
    )
    for a, column in zip(arrays, columns):
        share = out[..., at : at + column.shape[along]]
        outs.append(share.reshape(*share.shape[:along], *a.shape[along:]))
        at += column.shape[along]
    return tuple(outs)


def rotate(heads, places):
    half = heads.shape[-1] // 2
    freqs = rope_base ** (-(jnp.arange(half).astype(jnp.float32) * 2.0) / heads.shape[-1])
    angles = places[:, None, None] * freqs
    cosine = jnp.cos(angles)
    sine = jnp.sin(angles)
    first = heads[..., :half]
    second = heads[..., half:]
    return jnp.concatenate([first * cosine - second * sine, second * cosine + first * sine], -1)


def shards(tokens, norm_gain, w_qkv, w_out, cache_keys, cache_values, lengths, positions):
    seqs = tokens.shape[1]
    local_width = tokens.shape[2]
    rows = 2 * seqs
    group = H // KVH
    query_width = H * HD
    pair_width = KVH * HD
    scale = 1.0 / math.sqrt(HD)
    flat = tokens.reshape(rows, local_width)
    widened = flat.astype(jnp.float32)
    totals = of_everyone(jnp.sum(widened * widened, -1), "seq")
    local = (
        widened * lax.rsqrt(totals[:, None] / D + epsilon) * norm_gain.astype(jnp.float32)
    ).astype(jnp.bfloat16)
    normed = collect(local, "seq", 1)
    moved = lax.all_to_all(normed, "batch", split_axis=1, concat_axis=0, tiled=True)
    projected = summed_on_arrival(
        jnp.dot(moved, w_qkv, preferred_element_type=jnp.float32), "batch", 0
    ).astype(jnp.bfloat16)
    projected = collect(projected, "seq", 1)
    places = jnp.concatenate([positions, positions + 1]).astype(jnp.float32)
    queries = rotate(
        projected[:, :query_width].astype(jnp.float32).reshape(rows, H, HD), places
    ).astype(jnp.bfloat16)
    fresh_keys = rotate(
        projected[:, query_width : query_width + pair_width]
        .astype(jnp.float32)
        .reshape(rows, KVH, HD),
        places,
    ).astype(jnp.bfloat16)
    fresh_values = projected[:, query_width + pair_width :].reshape(2, seqs, KVH, HD)
    queries = queries.reshape(2, seqs, KVH, group, HD)
    fresh_keys = fresh_keys.reshape(2, seqs, KVH, HD)
    index = lax.axis_index("seq")
    shard_len = cache_keys.shape[1]
    keys_local = cache_keys.reshape(seqs, shard_len, KVH, HD)
    values_local = cache_values.reshape(seqs, shard_len, KVH, HD)
    scores = (
        jnp.einsum("tbkgd,bnkd->tbkgn", queries, keys_local, preferred_element_type=jnp.float32)
        * scale
    )
    extra_scores = (
        jnp.einsum("tbkgd,jbkd->tbkgj", queries, fresh_keys, preferred_element_type=jnp.float32)
        * scale
    )
    global_rows = index * shard_len + jnp.arange(shard_len)
    live_cache = (global_rows[None, :] < lengths[:, None])[None, :, None, None, :]
    steps_index = jnp.arange(2)
    owner = (lengths[:, None] + steps_index[None, :]) // shard_len == index
    causal = steps_index[None, :] <= steps_index[:, None]
    live_extra = (owner[None, :, :] & causal[:, None, :])[:, :, None, None, :]
    local_peak = jnp.maximum(
        jnp.max(jnp.where(live_cache, scores, lowest), -1),
        jnp.max(jnp.where(live_extra, extra_scores, lowest), -1),
    )
    weights = jnp.where(live_cache, jnp.exp(scores - local_peak[..., None]), 0.0)
    extra_weights = jnp.where(live_extra, jnp.exp(extra_scores - local_peak[..., None]), 0.0)
    total = jnp.sum(weights, -1) + jnp.sum(extra_weights, -1)
    summed = jnp.einsum(
        "tbkgn,bnkd->tbkgd",
        weights.astype(jnp.bfloat16),
        values_local,
        preferred_element_type=jnp.float32,
    )
    summed = summed + jnp.einsum(
        "tbkgj,jbkd->tbkgd",
        extra_weights.astype(jnp.bfloat16),
        fresh_values,
        preferred_element_type=jnp.float32,
    )
    summed = summed.reshape(rows, H, HD)
    total = total.reshape(rows, H)
    local_peak = local_peak.reshape(rows, H)
    parts_sum, parts_total, parts_peak = sent_together(
        (summed[None], total[None], local_peak[None]), "seq", 2, 0, 3
    )
    peak = jnp.max(parts_peak, 0, keepdims=True)
    factor = jnp.exp(parts_peak - peak)
    mine = jnp.sum(factor[..., None] * parts_sum, 0)
    mine_total = jnp.sum(factor * parts_total, 0)
    attended = (mine / mine_total[..., None]).astype(jnp.bfloat16).reshape(rows, -1)
    partial_value = jnp.dot(attended, w_out, preferred_element_type=jnp.float32)
    columns = summed_on_arrival(partial_value, "seq", 1)
    return (flat.astype(jnp.float32) + columns).astype(jnp.bfloat16).reshape(2, seqs, local_width)


def solution(mesh):
    return jax.shard_map(
        shards,
        mesh=mesh,
        in_specs=(
            P(None, "batch", "seq"),
            P("seq"),
            P("batch", "seq"),
            P("seq", None),
            P("batch", "seq", None),
            P("batch", "seq", None),
            P("batch"),
            P("batch"),
        ),
        out_specs=P(None, "batch", "seq"),
        check_vma=False,
    )
```

profile of v0, /device:TPU:1, one launch (start us, length us, event | category | flops | bytes accessed | tf_op | source)
XLA Modules:
  0.0 184.6 jit_solution(10569437129667557603)
XLA Ops:
  0.0 0.8 multiply_reduce_fusion
  0.8 0.1 broadcast_in_dim.45
  0.9 0.6 broadcast_in_dim.46
  1.6 10.3 %all-to-all-start = ((f32[64,1,32]{2,1,0:T(1,128)}), f32[64,1,32]{2,1,0:T(1,128)S(1)}, u32[]{:S(2)}, u32[]{:S(2)}) async-start(f32[64,1,32]{2,1,0:T(1,128)} %broadcast_in_dim.46), calls=%async_computation | async-start | bytes 65536 | tf_op jit(solution)/shard_map/all_to_all | solution.py:21
  11.9 0.7 convert_element_type.87
  12.6 7.1 %all-to-all-done = f32[64,1,32]{2,1,0:T(1,128)S(1)} async-done(((f32[64,1,32]{2,1,0:T(1,128)}), f32[64,1,32]{2,1,0:T(1,128)S(1)}, u32[]{:S(2)}, u32[]{:S(2)}) %all-to-all-start) | async-done | bytes 8224 | tf_op jit(solution)/shard_map/all_to_all | solution.py:21
  19.7 0.1 reduce_sum.77
  19.8 0.8 fusion.40
  20.5 0.1 broadcast_in_dim.47
  20.6 17.3 %all_to_all.60 = bf16[64,32,128]{2,1,0:T(8,128)(2,1)S(1)} all-to-all(bf16[64,32,128]{2,1,0:T(8,128)(2,1)S(1)} %broadcast_in_dim.47), channel_id=1, replica_groups=mesh['batch'=4,'seq'=64] {'seq'}, dimensions={0} | all-to-all | bytes 1048576 | tf_op jit(solution)/shard_map/all_to_all | solution.py:21
  37.9 0.2 copy.98
  38.1 0.1 all_to_all.43
  38.2 1.1 copy.99
  39.3 7.3 %all-to-all-start.2 = ((bf16[32,4,2048]{2,0,1:T(8,128)(2,1)}), bf16[32,4,2048]{2,0,1:T(8,128)(2,1)S(1)}, u32[]{:S(2)}, u32[]{:S(2)}) async-start(bf16[32,4,2048]{2,0,1:T(8,128)(2,1)} %copy.99), calls=%async_computation.2 | async-start | bytes 1048576 | tf_op jit(solution)/shard_map/all_to_all | solution.py:93
  46.6 0.1 fusion.42
  46.7 14.1 %all-to-all-done.2 = bf16[32,4,2048]{2,0,1:T(8,128)(2,1)S(1)} async-done(((bf16[32,4,2048]{2,0,1:T(8,128)(2,1)}), bf16[32,4,2048]{2,0,1:T(8,128)(2,1)S(1)}, u32[]{:S(2)}, u32[]{:S(2)}) %all-to-all-start.2) | async-done | bytes 524320 | tf_op jit(solution)/shard_map/all_to_all | solution.py:93
  60.9 1.0 fusion.20
  61.9 4.9 %all-to-all-start.3 = ((f32[4,32,160]{2,1,0:T(8,128)}), f32[4,32,160]{2,1,0:T(8,128)S(1)}, u32[]{:S(2)}, u32[]{:S(2)}) async-start(f32[4,32,160]{2,1,0:T(8,128)} %fusion.20), calls=%async_computation.3 | async-start | bytes 262144 | tf_op jit(solution)/shard_map/all_to_all | solution.py:48
  66.8 0.1 add_convert_fusion.3
  66.8 5.4 %copy.137 = bf16[256,8,8,128]{3,2,1,0:T(8,128)(2,1)} copy(bf16[256,8,8,128]{3,1,2,0:T(8,128)(2,1)} %bitcast.116) | data formatting | bytes 8388608
  72.2 3.1 %copy.139 = bf16[256,8,8,128]{3,2,1,0:T(8,128)(2,1)} copy(bf16[256,8,8,128]{3,1,2,0:T(8,128)(2,1)S(1)} %bitcast.117) | data formatting | bytes 8388608
  75.3 0.0 all-to-all-done.3
  75.3 1.2 broadcast_in_dim.48
  76.5 6.1 %all-to-all-start.4 = ((bf16[64,32,160]{2,1,0:T(8,128)(2,1)}), bf16[64,32,160]{2,1,0:T(8,128)(2,1)S(1)}, u32[]{:S(2)}, u32[]{:S(2)}) async-start(bf16[64,32,160]{2,1,0:T(8,128)(2,1)} %broadcast_in_dim.48), calls=%async_computation.4 | async-start | bytes 2097152 | tf_op jit(solution)/shard_map/all_to_all | solution.py:21
  82.6 0.1 broadcast_compare_fusion
  82.7 0.1 multiply_cosine_fusion
  82.8 4.7 %bitcast_bitcast_fusion.1 = bf16[16,128,8,128,1]{3,2,1,0,4:T(8,128)(2,1)} fusion(bf16[16,128,8,128]{3,2,1,0:T(8,128)(2,1)} %bitcast.108), kind=kLoop, calls=%fused_computation.1 | loop fusion | bytes 8388608 | tf_op jit(solution)/shard_map/reshape | solution.py:113
  87.5 2.2 %bitcast_bitcast_fusion = bf16[16,128,8,128,1]{3,2,1,0,4:T(8,128)(2,1)} fusion(bf16[16,128,8,128]{3,2,1,0:T(8,128)(2,1)S(1)} %bitcast.107), kind=kLoop, calls=%fused_computation | loop fusion | bytes 8388608 | tf_op jit(solution)/shard_map/reshape | solution.py:114
  89.8 10.9 %all-to-all-done.4 = bf16[64,32,160]{2,1,0:T(8,128)(2,1)S(1)} async-done(((bf16[64,32,160]{2,1,0:T(8,128)(2,1)}), bf16[64,32,160]{2,1,0:T(8,128)(2,1)S(1)}, u32[]{:S(2)}, u32[]{:S(2)}) %all-to-all-start.4) | async-done | bytes 655392 | tf_op jit(solution)/shard_map/all_to_all | solution.py:21
  100.7 0.6 copy.100
  101.3 1.7 reshape.412
  103.0 0.1 convert_bitcast_fusion
  103.1 0.2 copy.136
  103.3 0.5 subtract_convert_fusion
  103.9 0.1 subtract_convert_fusion.1
  104.0 0.1 copy.104
  104.1 0.1 copy.105
  104.2 1.3 copy-done.1
  105.5 2.5 %select_reduce_fusion = (f32[2,16,8,8]{3,0,2,1:T(2,128)S(1)}, f32[2,16,8,8,128]{4,3,0,2,1:T(8,128)S(1)}) fusion(pred[16,128]{1,0:T(8,128)(4,1)S(1)} %broadcast_compare_fusion, bf16[16,128,8,128,1]{3,2,1,0,4:T(8,128)(2,1)S(1)} %copy-done.1, bf16[2,16,8,8,64]{4,3,2,1,0:T(8,128)(2,1)S(1)} %bitcast.121, bf16[2,16,8,8,64]{4,3,2,1,0:T(8,128)(2,1)S(1)} %bitcast.119), kind=kOutput, calls=%fused_computation.19 | convolution fusion | flops 68941824 | bytes 5777408 | tf_op jit(solution)/shard_map/tbkgd,bnkd->tbkgn/dot_general | solution.py:116
  108.0 2.6 %select_reduce_fusion.1 = (f32[2,16,8,8]{3,0,2,1:T(2,128)S(1)}, f32[2,16,8,8,2]{3,4,0,2,1:T(2,128)S(1)}) fusion(pred[2,16,2]{2,0,1:T(4,128)(4,1)S(1)} %broadcast_and_fusion, bf16[2,16,8,64]{3,0,2,1:T(2,128)(2,1)S(1)} %copy.105, bf16[2,16,8,64]{3,0,2,1:T(2,128)(2,1)S(1)} %copy.104, bf16[2,16,8,8,64]{4,3,2,1,0:T(8,128)(2,1)S(1)} %bitcast.122, ...), kind=kOutput, calls=%fused_computation.34 | convolution fusion | flops 2238464 | bytes 614464 | tf_op jit(solution)/shard_map/tbkgd,jbkd->tbkgj/dot_general | solution.py:120
  110.6 0.1 max.17
  110.7 0.6 fusion.45
  111.3 0.5 convolution_bitcast_fusion.1
  111.8 0.8 fusion.18
  112.5 1.3 fusion.14
  113.8 0.1 copy.108
  113.9 0.1 add.83
  114.0 0.3 reshape.433
  114.3 1.3 reshape.434
  115.7 1.6 pad_maximum_fusion
  117.3 2.8 %copy.113 = f32[1,32,64,130]{3,1,0,2:T(8,128)} copy(f32[1,32,64,130]{3,2,1,0:T(8,128)S(1)} %pad_maximum_fusion) | data formatting | bytes 2129920 | tf_op jit(solution)/shard_map/concatenate | solution.py:54
  120.1 5.6 %all-to-all-start.5 = ((f32[1,32,64,130]{3,1,0,2:T(8,128)}), f32[1,32,64,130]{3,1,0,2:T(8,128)}, u32[]{:S(2)}, u32[]{:S(2)}) async-start(f32[1,32,64,130]{3,1,0,2:T(8,128)} %copy.113), calls=%async_computation.5 | async-start | bytes 4194304 | tf_op jit(solution)/shard_map/all_to_all | solution.py:56
  125.7 2.5 %copy.132 = bf16[8192,128]{1,0:T(8,128)(2,1)} copy(bf16[8192,128]{0,1:T(8,128)(2,1)S(1)} %bitcast.123) | data formatting | bytes 4194304 | tf_op jit(solution)/shard_map/dot_general | solution.py:159
  128.1 27.1 %all-to-all-done.5 = f32[1,32,64,130]{3,1,0,2:T(8,128)} async-done(((f32[1,32,64,130]{3,1,0,2:T(8,128)}), f32[1,32,64,130]{3,1,0,2:T(8,128)}, u32[]{:S(2)}, u32[]{:S(2)}) %all-to-all-start.5) | async-done | bytes 1064992 | tf_op jit(solution)/shard_map/all_to_all | solution.py:56
  155.3 3.3 %copy.114 = f32[1,32,64,130]{2,1,3,0:T(8,128)S(1)} copy(f32[1,32,64,130]{3,1,0,2:T(8,128)} %all-to-all-done.5) | data formatting | bytes 2129920 | tf_op jit(solution)/shard_map/all_to_all | solution.py:56
  158.6 0.1 slice_reduce_fusion
  158.7 0.2 fusion.37
  158.9 0.1 exponential_bitcast_fusion
  159.0 0.6 fusion.4
  159.6 0.6 copy-done.3
  160.2 0.8 convolution_bitcast_fusion
  161.0 22.9 %all_to_all.61 = f32[64,32,128]{2,1,0:T(8,128)S(1)} all-to-all(f32[64,32,128]{2,1,0:T(8,128)S(1)} %convolution_bitcast_fusion), channel_id=1, replica_groups=mesh['batch'=4,'seq'=64] {'seq'}, dimensions={0} | all-to-all | bytes 2097152 | tf_op jit(solution)/shard_map/all_to_all | solution.py:48
  183.9 0.1 reduce_sum.84
  184.0 0.6 add_convert_fusion.2
  (31 shorter events, 0.2 us)
Async XLA Ops:
  0.0 60.9 %copy-start = (bf16[2048,160]{0,1:T(8,128)(2,1)S(1)}, bf16[2048,160]{0,1:T(8,128)(2,1)}, u32[]{:S(2)}) copy-start(bf16[2048,160]{0,1:T(8,128)(2,1)} %param.10) | copy-start | bytes 1966084
  1.6 18.1 %all-to-all-start = ((f32[64,1,32]{2,1,0:T(1,128)}), f32[64,1,32]{2,1,0:T(1,128)S(1)}, u32[]{:S(2)}, u32[]{:S(2)}) async-start(f32[64,1,32]{2,1,0:T(1,128)} %broadcast_in_dim.46), calls=%async_computation | async-start | bytes 65536 | tf_op jit(solution)/shard_map/all_to_all | solution.py:21
  37.9 8.7 %copy-start.9 = (s32[16]{0:T(128)S(1)}, s32[16]{0:T(128)}, u32[]{:S(2)}) copy-start(s32[16]{0:T(128)} %param.15) | copy-start | bytes 196
  37.9 8.7 %copy-start.8 = (s32[16]{0:T(128)S(1)}, s32[16]{0:T(128)}, u32[]{:S(2)}) copy-start(s32[16]{0:T(128)} %param.14) | copy-start | bytes 196
  39.3 21.6 %all-to-all-start.2 = ((bf16[32,4,2048]{2,0,1:T(8,128)(2,1)}), bf16[32,4,2048]{2,0,1:T(8,128)(2,1)S(1)}, u32[]{:S(2)}, u32[]{:S(2)}) async-start(bf16[32,4,2048]{2,0,1:T(8,128)(2,1)} %copy.99), calls=%async_computation.2 | async-start | bytes 1048576 | tf_op jit(solution)/shard_map/all_to_all | solution.py:93
  61.9 13.4 %all-to-all-start.3 = ((f32[4,32,160]{2,1,0:T(8,128)}), f32[4,32,160]{2,1,0:T(8,128)S(1)}, u32[]{:S(2)}, u32[]{:S(2)}) async-start(f32[4,32,160]{2,1,0:T(8,128)} %fusion.20), calls=%async_computation.3 | async-start | bytes 262144 | tf_op jit(solution)/shard_map/all_to_all | solution.py:48
  66.8 5.4 %copy-start.4 = (bf16[16,128,1024]{2,1,0:T(8,128)(2,1)S(1)}, bf16[16,128,1024]{2,1,0:T(8,128)(2,1)}, u32[]{:S(2)}) copy-start(bf16[16,128,1024]{2,1,0:T(8,128)(2,1)} %param.13) | copy-start | bytes 12582916
  76.5 24.2 %all-to-all-start.4 = ((bf16[64,32,160]{2,1,0:T(8,128)(2,1)}), bf16[64,32,160]{2,1,0:T(8,128)(2,1)S(1)}, u32[]{:S(2)}, u32[]{:S(2)}) async-start(bf16[64,32,160]{2,1,0:T(8,128)(2,1)} %broadcast_in_dim.48), calls=%async_computation.4 | async-start | bytes 2097152 | tf_op jit(solution)/shard_map/all_to_all | solution.py:21
  82.8 4.7 %copy-start.2 = (bf16[256,8,8,128]{3,2,1,0:T(8,128)(2,1)S(1)}, bf16[256,8,8,128]{3,2,1,0:T(8,128)(2,1)}, u32[]{:S(2)}) copy-start(bf16[256,8,8,128]{3,2,1,0:T(8,128)(2,1)} %copy.139) | copy-start | bytes 12582916
  103.3 2.2 %copy-start.1 = (bf16[16,128,8,128,1]{3,2,1,0,4:T(8,128)(2,1)S(1)}, bf16[16,128,8,128,1]{3,2,1,0,4:T(8,128)(2,1)}, u32[]{:S(2)}) copy-start(bf16[16,128,8,128,1]{3,2,1,0,4:T(8,128)(2,1)} %bitcast_bitcast_fusion.1) | copy-start | bytes 12582916
  108.0 4.6 %copy-start.5 = (bf16[16,128,8,128,1]{3,2,1,0,4:T(8,128)(2,1)S(1)}, bf16[16,128,8,128,1]{3,2,1,0,4:T(8,128)(2,1)}, u32[]{:S(2)}) copy-start(bf16[16,128,8,128,1]{3,2,1,0,4:T(8,128)(2,1)} %bitcast_bitcast_fusion) | copy-start | bytes 12582916
  120.0 5.6 %copy-start.6 = (bf16[128,8192]{1,0:T(8,128)(2,1)S(1)}, bf16[128,8192]{1,0:T(8,128)(2,1)}, u32[]{:S(2)}) copy-start(bf16[128,8192]{1,0:T(8,128)(2,1)} %param.11) | copy-start | bytes 6291460
  120.1 35.2 %all-to-all-start.5 = ((f32[1,32,64,130]{3,1,0,2:T(8,128)}), f32[1,32,64,130]{3,1,0,2:T(8,128)}, u32[]{:S(2)}, u32[]{:S(2)}) async-start(f32[1,32,64,130]{3,1,0,2:T(8,128)} %copy.113), calls=%async_computation.5 | async-start | bytes 4194304 | tf_op jit(solution)/shard_map/all_to_all | solution.py:56
  158.6 1.6 copy-start.3
  161.0 23.0 %copy-start.7 = (bf16[2,16,128]{2,1,0:T(8,128)(2,1)S(1)}, bf16[2,16,128]{2,1,0:T(8,128)(2,1)}, u32[]{:S(2)}) copy-start(bf16[2,16,128]{2,1,0:T(8,128)(2,1)} %param.8) | copy-start | bytes 24580
where the time goes:
time: 185 us
  waiting for transfers between devices  59.3 us (32%)
  blocking collectives  40.1 us (22%)
  starting transfers between devices  34.2 us (18%)
  local copies, waits for them, and re-layouts  33.6 us (18%)
  matrix products  8.71 us (5%)
  other arithmetic  8.36 us (5%)
    all_to_all x1, waiting for transfers between devices, sent_together(): lax.all_to_all(both, axis, split_axis=split_dim, concat_axis=concat_dim,...  27.1 us
    all_to_all x1, blocking collectives, summed_on_arrival(): lax.all_to_all(split_up(array, dim, devices), axis, 0, 0, tiled=True)  22.9 us
    all_to_all x2, waiting for transfers between devices, sent_to_all(): lax.all_to_all(jnp.broadcast_to(array[None], (devices, *array.shape)), ax...  18.1 us
    all_to_all x1, blocking collectives, sent_to_all(): lax.all_to_all(jnp.broadcast_to(array[None], (devices, *array.shape)), ax...  17.3 us
    all_to_all x2, starting transfers between devices, sent_to_all(): lax.all_to_all(jnp.broadcast_to(array[None], (devices, *array.shape)), ax...  16.4 us
    all_to_all x1, waiting for transfers between devices, shards(): lax.all_to_all(normed, 'batch', split_axis=1, concat_axis=0, tiled=True)  14.1 us
    unnamed x25, local copies, waits for them, and re-layouts  10.6 us
    all_to_all x1, starting transfers between devices, shards(): lax.all_to_all(normed, 'batch', split_axis=1, concat_axis=0, tiled=True)  7.28 us
  transfers between devices with their start and end apart: 5, of which 4 were waited for; matrix products, arithmetic and copies ran while one was open for 10% of the time, Pallas kernels for 0%

commit v1 on v0

v1 whole, which is shorter than its diff:
```python
import functools
import math

import jax
import jax.numpy as jnp
from jax import lax
from jax.experimental import pallas as pl
from jax.experimental.pallas import tpu as pltpu
from jax.sharding import PartitionSpec as P

D = 8192
H = 64
KVH = 8
HD = 128
MESH = pl.DeviceIdType.MESH

rope_base = 500000.0
epsilon = 1e-05
lowest = -1e30


def gray(i):
    return i ^ (i >> 1)


def kernel(
    tok, gain, cosine, sine, lens, wq_hbm, wo_hbm, k_hbm, v_hbm, out,
    wq, wo, kc, vc,
    sq_out, sq_in, x_in, a_out, a_in, xn,
    part, p_in, q_out, g_in, q32,
    o32, o_out, st_out, o_in, st_in, fac, y_out, y_in,
    hbm_sem, s1_send, s1_recv, sq_send, sq_recv, x_send, x_direct, xf_send, x_fwd, a_send, a_recv,
    p_send, p_recv, g_send, g_direct, gf_send, g_fwd,
    o_send, o_recv, st_send, st_recv, y_send, y_recv,
):
    b = lax.axis_index("batch")
    s = lax.axis_index("seq")
    c = s % 2
    zl = (s // 2) % 2
    x = (s // 4) % 4
    y = s // 16
    m = s % 4
    q = s // 4
    j16 = s % 16
    partner = s + 1 - 2 * c

    def remote(src, dst, send, recv, bb, ss):
        return pltpu.make_async_remote_copy(
            src_ref=src, dst_ref=dst, send_sem=send, recv_sem=recv,
            device_id=(bb, ss), device_id_type=MESH,
        )

    def take(sem, ref):
        pltpu.make_async_copy(ref, ref, sem).wait()

    loads = [
        pltpu.make_async_copy(src, dst, hbm_sem.at[i])
        for i, (src, dst) in enumerate(((wq_hbm, wq), (k_hbm, kc), (v_hbm, vc), (wo_hbm, wo)))
    ]
    for load in loads:
        load.start()

    bar = pltpu.get_barrier_semaphore()

    def greet(bb, ss):
        pl.semaphore_signal(bar, inc=1, device_id=(bb, ss), device_id_type=MESH)

    def greet_near(i, _):
        db = 1 + i // 4
        greet((b + db) % 4, ((y + i % 4) % 4) * 16 + j16)
        return 0

    lax.fori_loop(0, 12, greet_near, 0)

    def greet_column(i, _):
        greet((b + 1 + i // 3) % 4, q * 4 + (m + 1 + i % 3) % 4)
        return 0

    lax.fori_loop(0, 9, greet_column, 0)

    def greet_group(i, _):
        greet(b, (s + i) % 64)
        return 0

    lax.fori_loop(1, 64, greet_group, 0)

    widened = tok[...].astype(jnp.float32)
    squares = jnp.concatenate([widened * widened] * 4, axis=0)
    row_group = lax.broadcasted_iota(jnp.int32, (128, 128), 0) // 32
    squares = jnp.where(row_group == b, squares, 0.0)
    sq_out[0:1, :] = jnp.sum(squares.T, axis=0, keepdims=True)
    sq_out[1:2, :] = gain[...].astype(jnp.float32)
    my_rows = pl.ds(pl.multiple_of(b * 32, 32), 32)
    sq_in[y * 4 + b] = sq_out[...]

    @pl.when(b == y)
    def _():
        x_in[j16, my_rows, :] = tok[...]

    q32[pl.ds(80 * 32, 128), :] = jnp.zeros((128, 128), jnp.float32)

    pl.semaphore_wait(bar, 84)

    def send_rows(i, _):
        yy = (y + 3 - i) % 4

        @pl.when((b != y) | (yy != y))
        def _():
            remote(
                tok, x_in.at[j16, my_rows], s1_send, s1_recv.at[b], y, yy * 16 + j16
            ).start()

        return 0

    lax.fori_loop(0, 4, send_rows, 0)

    def send_squares(i, _):
        remote(
            sq_out, sq_in.at[y * 4 + b], sq_send, sq_recv,
            (b + i // 4) % 4, ((y + i % 4) % 4) * 16 + j16,
        ).start()
        return 0

    lax.fori_loop(1, 16, send_squares, 0)

    for i, off in enumerate((0, 1, 3, 2)):
        bb = (b + off) % 4
        piece = x_in.at[j16, pl.ds(pl.multiple_of(bb * 32, 32), 32)]
        if off == 0:
            @pl.when(b != y)
            def _():
                take(s1_recv.at[bb], piece)
        else:
            take(s1_recv.at[bb], piece)

        def send_piece(t, _):
            tt = 7 - t
            xx = (x + gray(tt // 2)) % 4
            zz = (zl + tt) % 2
            cc = jnp.where(tt == 0, 1 - c, c)
            remote(
                piece, piece, x_send, x_direct.at[j16], b, ((y * 4 + xx) * 2 + zz) * 2 + cc
            ).start()
            return 0

        lax.fori_loop(0, 8, send_piece, 0)

    take(sq_recv, sq_in.at[pl.ds(0, 15)])
    a_out[0:1, :] = jnp.sum(sq_in[:, 0:1, :], axis=0)
    a_out[1:2, :] = sq_in[b * 4 + b][1:2, :]
    a_in[j16] = a_out[...]

    def send_stats(i, _):
        remote(
            a_out, a_in.at[j16], a_send, a_recv, b, y * 16 + (j16 + i) % 16
        ).start()
        return 0

    lax.fori_loop(1, 16, send_stats, 0)

    def forward_block(t, _):
        xx = (x + gray(t // 2)) % 4
        zz = (zl + t) % 2
        jj = (xx * 2 + zz) * 2 + c
        block = x_in.at[jj]
        take(x_direct.at[jj], block)
        remote(block, block, xf_send, x_fwd, b, partner).start()
        return 0

    lax.fori_loop(1, 8, forward_block, 0)
    jp = j16 + 1 - 2 * c
    take(x_direct.at[jp], x_in.at[jp])
    take(x_fwd, x_in.at[pl.ds(0, 7)])
    take(a_recv, a_in.at[pl.ds(0, 15)])

    totals = jnp.sum(a_in[:, 0:1, :], axis=0)
    inverse = lax.rsqrt(totals / D + epsilon)
    inverse = jnp.broadcast_to(inverse, (128, 128)).T
    for j in range(16):
        xn[:, j * 128 : (j + 1) * 128] = (
            x_in[j].astype(jnp.float32) * inverse * a_in[j][1:2, :]
        ).astype(jnp.bfloat16)
    loads[0].wait()
    product = jnp.dot(xn[...], wq[...], preferred_element_type=jnp.float32)
    product = jnp.concatenate([product, jnp.zeros((128, 96), jnp.float32)], axis=1)
    product = pltpu.roll(product, 32 * m, 1)
    part[...] = product.reshape(16, 8, 256)
    p_in[b * 4 + m] = part[b * 4 + m]

    def send_part(i, _):
        bb = (b + gray(3 - i // 4)) % 4
        mm = (m + 3 - i % 4) % 4
        remote(
            part.at[bb * 4 + mm], p_in.at[b * 4 + m], p_send, p_recv, bb, q * 4 + mm
        ).start()
        return 0

    lax.fori_loop(0, 15, send_part, 0)
    take(p_recv, p_in.at[pl.ds(0, 15)])

    rows8 = pl.ds(pl.multiple_of(m * 8, 8), 8)
    cos8 = cosine[rows8, :]
    sin8 = sine[rows8, :]
    sums = [p_in[mm] + p_in[4 + mm] + p_in[8 + mm] + p_in[12 + mm] for mm in range(4)]
    for j in range(5):
        head = None
        if j < 4:
            head = sums[j][:, :128]
        if j > 0:
            upper = sums[j - 1][:, 128:]
            head = upper if head is None else head + upper
        head = head.astype(jnp.bfloat16).astype(jnp.float32)
        turned = head * cos8 + pltpu.roll(head, 64, 1) * sin8
        q_out[j] = jnp.where(q * 5 + j < H + KVH, turned, head).astype(jnp.bfloat16)
    g_in[s] = q_out[...]

    def chip_at(t):
        yy = (y + gray(t // 8)) % 4
        xx = (x + gray((t // 2) % 4)) % 4
        zz = (zl + t) % 2
        return ((yy * 4 + xx) * 2 + zz) * 2

    def send_heads(t, _):
        tt = 31 - t
        cc = jnp.where(tt == 0, 1 - c, c)
        remote(q_out, g_in.at[s], g_send, g_direct.at[s], b, chip_at(tt) + cc).start()
        return 0

    lax.fori_loop(0, 32, send_heads, 0)

    def forward_heads(t, _):
        ss = chip_at(t) + c
        block = g_in.at[ss]
        take(g_direct.at[ss], block)
        remote(block, block, gf_send, g_fwd, b, partner).start()
        return 0

    lax.fori_loop(1, 32, forward_heads, 0)
    take(g_direct.at[partner], g_in.at[partner])
    take(g_fwd, g_in.at[pl.ds(0, 31)])

    def spread(qq, _):
        for mm in range(4):
            block = g_in[qq * 4 + mm].astype(jnp.float32)
            for j in range(5):
                at = pl.multiple_of((qq * 5 + j) * 32 + mm * 8, 8)
                q32[pl.ds(at, 8), :] = block[j]
        return 0

    lax.fori_loop(0, 16, spread, 0)

    loads[1].wait()
    loads[2].wait()
    scale = 1.0 / math.sqrt(HD)
    lane = lax.broadcasted_iota(jnp.int32, (16, 128), 1)
    step = lax.broadcasted_iota(jnp.int32, (16, 128), 0) // 8
    lane8 = lax.broadcasted_iota(jnp.int32, (8, 128), 1)

    def attend(i, _):
        k = (i + s // 8) % 8
        cols = pl.ds(pl.multiple_of(k * 128, 128), 128)
        queries = []
        for bs in range(16):
            for t in range(2):
                queries.append(q32[pl.ds(k * 256 + t * 16 + bs, 8, stride=32), :])
        queries = jnp.concatenate(queries, axis=0).astype(jnp.bfloat16)
        fresh_at = pl.multiple_of((H + k) * 32, 32)
        fresh_keys = q32[pl.ds(fresh_at, 128), :].astype(jnp.bfloat16)
        fresh_at = pl.multiple_of((H + KVH + k) * 32, 32)
        fresh_values = q32[pl.ds(fresh_at, 128), :].astype(jnp.bfloat16)
        over = (((1,), (1,)), ((), ()))
        extra_all = lax.dot_general(
            queries, fresh_keys, over, preferred_element_type=jnp.float32
        )
        stats = jnp.zeros((8, 128), jnp.float32)
        extra_weights = []
        sums_of = []
        for bs in range(16):
            length = lens[bs]
            rows = slice(bs * 16, bs * 16 + 16)
            scores = (
                lax.dot_general(
                    queries[rows], kc[bs, :, cols], over, preferred_element_type=jnp.float32
                )
                * scale
            )
            live = lane < length - s * 128
            which = lane // 16
            live_extra = (
                (lane % 16 == bs) & (which <= step) & (lane < 32) & ((length + which) // 128 == s)
            )
            scores = jnp.where(live, scores, lowest)
            extra = jnp.where(live_extra, extra_all[rows] * scale, lowest)
            peak = jnp.max(jnp.maximum(scores, extra), axis=1, keepdims=True)
            weights = jnp.where(live, jnp.exp(scores - peak), 0.0)
            weights_extra = jnp.where(live_extra, jnp.exp(extra - peak), 0.0)
            total = jnp.sum(weights + weights_extra, axis=1, keepdims=True)
            extra_weights.append(weights_extra.astype(jnp.bfloat16))
            sums_of.append(
                jnp.dot(
                    weights.astype(jnp.bfloat16), vc[bs, :, cols], preferred_element_type=jnp.float32
                )
            )
            for t in range(2):
                stats = jnp.where(lane8 == t * 16 + bs, total[t * 8 : t * 8 + 8], stats)
                stats = jnp.where(lane8 == 32 + t * 16 + bs, peak[t * 8 : t * 8 + 8], stats)
        extra_sums = jnp.dot(
            jnp.concatenate(extra_weights, axis=0), fresh_values, preferred_element_type=jnp.float32
        )
        for bs in range(16):
            for t in range(2):
                at = bs * 16 + t * 8
                o32[pl.ds(t * 16 + bs, 8, stride=32), :] = (
                    sums_of[bs][t * 8 : t * 8 + 8] + extra_sums[at : at + 8]
                )
        for g in range(8):
            o_out[k * 8 + g] = o32[g * 32 : g * 32 + 32, :].astype(jnp.bfloat16)
            st_out[k * 8 + g] = stats[g : g + 1]

        def send_sums(g, _):
            h = k * 8 + g

            @pl.when(h != s)
            def _():
                remote(o_out.at[h], o_in.at[s], o_send, o_recv, b, h).start()
                remote(st_out.at[h], st_in.at[s], st_send, st_recv, b, h).start()

            return 0

        lax.fori_loop(0, 8, send_sums, 0)
        return 0

    lax.fori_loop(0, 8, attend, 0)
    o_in[s] = o_out[s]
    st_in[s] = st_out[s]
    take(st_recv, st_in.at[pl.ds(0, 63)])

    peak = st_in[0]
    for i in range(1, 64):
        peak = jnp.maximum(peak, st_in[i])
    total = jnp.zeros((1, 128), jnp.float32)
    lane1 = lax.broadcasted_iota(jnp.int32, (1, 128), 1)
    for i in range(64):
        row = st_in[i]
        factor = jnp.where((lane1 >= 32) & (lane1 < 64), jnp.exp(row - peak), 0.0)
        fac[i : i + 1, :] = factor
        total = total + factor * pltpu.roll(row, 32, 1)
    fac[64:65, :] = total
    fac[65:128, :] = jnp.zeros((63, 128), jnp.float32)
    factors = fac[...].T[32:64, :]
    take(o_recv, o_in.at[pl.ds(0, 63)])
    summed = jnp.zeros((32, 128), jnp.float32)
    for i in range(64):
        summed = summed + factors[:, i : i + 1] * o_in[i].astype(jnp.float32)
    attended = (summed / factors[:, 64:65]).astype(jnp.bfloat16)

    loads[3].wait()

    def mix(i, _):
        chunk = (i + q + 10) % 16
        cols = pl.ds(pl.multiple_of(chunk * 512, 512), 512)
        values = jnp.dot(attended, wo[:, cols], preferred_element_type=jnp.float32)
        for u in range(4):
            y_out[chunk * 4 + u] = values[:, u * 128 : (u + 1) * 128].astype(jnp.bfloat16)

        def send_mixed(u, _):
            d = chunk * 4 + u

            @pl.when(d != s)
            def _():
                remote(y_out.at[d], y_in.at[s], y_send, y_recv, b, d).start()

            return 0

        lax.fori_loop(0, 4, send_mixed, 0)
        return 0

    lax.fori_loop(0, 16, mix, 0)
    y_in[s] = y_out[s]
    take(y_recv, y_in.at[pl.ds(0, 63)])
    mixed = tok[...].astype(jnp.float32)
    added = jnp.zeros((32, 128), jnp.float32)
    for i in range(64):
        added = added + y_in[i].astype(jnp.float32)
    out[...] = (mixed + added).astype(jnp.bfloat16)

    @pl.when(b != y)
    def _():
        take(s1_send, x_in.at[0])

    @pl.when(b == y)
    def _():
        take(s1_send, x_in.at[0, pl.ds(0, 96)])

    take(sq_send, sq_in.at[pl.ds(0, 15)])
    take(x_send, x_in.at[pl.ds(0, 8)])
    take(xf_send, x_in.at[pl.ds(0, 7)])
    take(a_send, a_in.at[pl.ds(0, 15)])
    take(p_send, p_in.at[pl.ds(0, 15)])
    take(g_send, g_in.at[pl.ds(0, 32)])
    take(gf_send, g_in.at[pl.ds(0, 31)])
    take(o_send, o_in.at[pl.ds(0, 63)])
    take(st_send, st_in.at[pl.ds(0, 63)])
    take(y_send, y_in.at[pl.ds(0, 63)])


def shards(tokens, norm_gain, w_qkv, w_out, cache_keys, cache_values, lengths, positions):
    seqs = tokens.shape[1]
    local_width = tokens.shape[2]
    rows = 2 * seqs
    places = jnp.concatenate([positions, positions + 1]).astype(jnp.float32)
    half = HD // 2
    freqs = rope_base ** (-(jnp.arange(half).astype(jnp.float32) * 2.0) / HD)
    angles = places[:, None] * freqs
    cosine = jnp.cos(angles)
    sine = jnp.sin(angles)
    cosine = jnp.concatenate([cosine, cosine], axis=1)
    sine = jnp.concatenate([-sine, sine], axis=1)
    f32, bf16 = jnp.float32, jnp.bfloat16
    vmem, dma = pltpu.VMEM, pltpu.SemaphoreType.DMA
    whole = pl.BlockSpec(memory_space=pltpu.VMEM)
    hbm = pl.BlockSpec(memory_space=pl.ANY)
    out = pl.pallas_call(
        kernel,
        out_shape=jax.ShapeDtypeStruct((rows, local_width), bf16),
        in_specs=[whole] * 4 + [pl.BlockSpec(memory_space=pltpu.SMEM)] + [hbm] * 4,
        out_specs=whole,
        scratch_shapes=[
            vmem(w_qkv.shape, bf16),
            vmem(w_out.shape, bf16),
            vmem(cache_keys.shape, bf16),
            vmem(cache_values.shape, bf16),
            vmem((2, 128), f32),
            vmem((16, 2, 128), f32),
            vmem((16, 128, 128), bf16),
            vmem((2, 128), f32),
            vmem((16, 2, 128), f32),
            vmem((128, 2048), bf16),
            vmem((16, 8, 256), f32),
            vmem((16, 8, 256), f32),
            vmem((5, 8, 128), bf16),
            vmem((64, 5, 8, 128), bf16),
            vmem((84 * 32, 128), f32),
            vmem((256, 128), f32),
            vmem((64, 32, 128), bf16),
            vmem((64, 1, 128), f32),
            vmem((64, 32, 128), bf16),
            vmem((64, 1, 128), f32),
            vmem((128, 128), f32),
            vmem((64, 32, 128), bf16),
            vmem((64, 32, 128), bf16),
            dma((4,)),
            dma, dma((4,)), dma, dma, dma, dma((16,)), dma, dma, dma, dma,
            dma, dma, dma, dma((64,)), dma, dma,
            dma, dma, dma, dma, dma, dma,
        ],
        compiler_params=pltpu.CompilerParams(
            collective_id=0, has_side_effects=True, vmem_limit_bytes=60 * 1024 * 1024
        ),
        name="layer",
    )(
        tokens.reshape(rows, local_width), norm_gain.reshape(1, local_width), cosine, sine, lengths,
        w_qkv, w_out, cache_keys, cache_values,
    )
    return out.reshape(2, seqs, local_width)


def solution(mesh):
    return jax.shard_map(
        shards,
        mesh=mesh,
        in_specs=(
            P(None, "batch", "seq"),
            P("seq"),
            P("batch", "seq"),
            P("seq", None),
            P("batch", "seq", None),
            P("batch", "seq", None),
            P("batch"),
            P("batch"),
        ),
        out_specs=P(None, "batch", "seq"),
        check_vma=False,
    )
```

time: 185 us -> 89.3 us (0.48)
  Pallas kernels: 0 us -> 83.3 us
  waiting for transfers between devices: 59.3 us -> 0 us
  blocking collectives: 40.1 us -> 0 us
  starting transfers between devices: 34.2 us -> 0 us
  local copies, waits for them, and re-layouts: 33.6 us -> 3.48 us
  matrix products: 8.71 us -> 0 us
  other arithmetic: 8.36 us -> 2.23 us
    pallas_call x0 -> x1, Pallas kernels: none -> 83.3 us  [shards(): pl.pallas_call(kernel, out_shape=jax.ShapeDtypeStruct((rows, local_width)...]
    all_to_all x5 -> x0, waiting for transfers between devices: 59.3 us -> none  [the longest x1 27.1 us: sent_together(): lax.all_to_all(both, axis, split_axis=split_dim, concat_axis=concat_dim,...]
    all_to_all x2 -> x0, blocking collectives: 40.1 us -> none  [the longest x1 22.9 us: summed_on_arrival(): lax.all_to_all(split_up(array, dim, devices), axis, 0, 0, tiled=True)]
    all_to_all x5 -> x0, starting transfers between devices: 34.2 us -> none  [the longest x2 16.4 us: sent_to_all(): lax.all_to_all(jnp.broadcast_to(array[None], (devices, *array.shape)), ax...]
    dot_general x6 -> x0, matrix products: 8.71 us -> none  [the longest x1 2.62 us: shards(): jnp.einsum('tbkgd,jbkd->tbkgj', queries, fresh_keys, preferred_element_ty...]
    reshape x4 -> x0, local copies, waits for them, and re-layouts: 8.62 us -> none  [the longest x1 4.71 us: shards(): keys_local = cache_keys.reshape(seqs, shard_len, KVH, HD)]
    unnamed x25 -> x2, local copies, waits for them, and re-layouts: 10.6 us -> 3.48 us
    all_to_all x3 -> x0, local copies, waits for them, and re-layouts: 4.52 us -> none  [the longest x1 3.32 us: sent_together(): lax.all_to_all(both, axis, split_axis=split_dim, concat_axis=concat_dim,...]
  transfers between devices with their start and end apart: 5 -> 0, of which waited for: 4 -> 0; matrix products, arithmetic and copies ran while one was open for 10% -> 0% of each run, Pallas kernels for 0% -> 0%
where the time goes in v1:
time: 89.3 us; the launch traced here: 89.1 us
  Pallas kernels  83.3 us (93%)
  local copies, waits for them, and re-layouts  3.48 us (4%)
  other arithmetic  2.23 us (2%)
    pallas_call x1, Pallas kernels, shards(): pl.pallas_call(kernel, out_shape=jax.ShapeDtypeStruct((rows, local_width)...  83.3 us
    unnamed x2, local copies, waits for them, and re-layouts  3.48 us

profile of v1, /device:TPU:1, one launch (start us, length us, event | category | flops | bytes accessed | tf_op | source)
XLA Modules:
  0.0 89.1 jit_solution(18113520887679163630)
XLA Ops:
  0.0 0.7 broadcast_add_fusion
  0.7 0.7 add_convert_fusion
  1.4 0.1 fusion
  1.5 0.7 pad_maximum_fusion
  2.2 2.2 %copy.9.wq_hbm = bf16[2048,160]{1,0:T(8,128)(2,1)} copy(bf16[2048,160]{0,1:T(8,128)(2,1)} %param.10) | data formatting | bytes 1310720 | tf_op args[2]
  4.4 83.3 %layer.1 = bf16[32,128]{1,0:T(8,128)(2,1)} custom-call(bf16[32,128]{1,0:T(8,128)(2,1)} %bitcast.4, bf16[1,128]{1,0:T(2,128)(2,1)} %bitcast.5, f32[32,128]{1,0:T(8,128)} %get-tuple-element.8.cosine, f32[32,128]{1,0:T(8,128)} %get-tuple-element.9.sine, s32[16]{0:T(128)} %lens.1, bf16[2048,160]{1,0:T(8,128)(2,1)} %copy.9.wq_hbm, bf16[128,8192]{1,0:T(8,128)(2,1)} %wo_hbm.1, ...), custom_call_target="tpu_custom_call" | custom-call | tf_op jit(solution)/shard_map/layer/pallas_call | solution.py:423
  87.8 1.3 %copy.11 = bf16[2,16,128]{2,1,0:T(8,128)(2,1)} copy(bf16[2,16,128]{2,1,0:T(8,128)(2,1)} %bitcast.3) | data formatting | bytes 16384
  (1 shorter events, 0.0 us)

commit v2 on v1

v2 whole, which is shorter than its diff:
```python
import math

import jax
import jax.numpy as jnp
import numpy as np
from jax import lax
from jax.experimental import pallas as pl
from jax.experimental.pallas import tpu as pltpu
from jax.sharding import PartitionSpec as P

D = 8192
H = 64
KVH = 8
HD = 128
MESH = pl.DeviceIdType.MESH

rope_base = 500000.0
epsilon = 1e-05
lowest = -1e30
floor = -1e29


def gray(i):
    return i ^ (i >> 1)


def kernel(
    tok, gain, freqs, lens, places, wq_hbm, wo_hbm, k_hbm, v_hbm, out,
    wq, wo, kc, vc,
    sq_out, sq_in, x_in, a_out, a_in, xn,
    part, p_in, q_out, g_in, q32,
    dead, dead_extra, raw, raw_extra, wts, wts_extra, peaks, sums, own,
    o32, o_out, st_out, o_in, st_in, fac, att, y_out, y_in,
    hbm_sem, swap_send, swap_recv,
    s1_send, s1_recv, sq_send, sq_recv, x_send, x_direct, xf_send, x_fwd, a_send, a_recv,
    p_send, p_recv, g_send, g_direct, gf_send, g_fwd,
    o_send, o_recv, st_send, st_recv, pair_recv, att_send, att_recv, y_send, y_recv,
):
    b = lax.axis_index("batch")
    s = lax.axis_index("seq")
    c = s % 2
    zl = (s // 2) % 2
    x = (s // 4) % 4
    y = s // 16
    m = s % 4
    q = s // 4
    j16 = s % 16
    partner = s + 1 - 2 * c
    half = s // 32
    chip = s // 2

    def remote(src, dst, send, recv, bb, ss):
        return pltpu.make_async_remote_copy(
            src_ref=src, dst_ref=dst, send_sem=send, recv_sem=recv,
            device_id=(bb, ss), device_id_type=MESH,
        )

    def take(sem, ref):
        pltpu.make_async_copy(ref, ref, sem).wait()

    def halves(cc):
        cols = pl.ds(pl.multiple_of(cc * 512, 512), 512)
        wide = pl.ds(pl.multiple_of(cc * 4096, 4096), 4096)
        return (
            (k_hbm.at[:, :, cols], kc.at[c]),
            (v_hbm.at[:, :, cols], vc.at[c]),
            (wo_hbm.at[:, wide], wo.at[c]),
        )

    loads = [
        pltpu.make_async_copy(src, dst, hbm_sem.at[i])
        for i, (src, dst) in enumerate(((wq_hbm, wq), *halves(c)))
    ]
    swaps = [
        remote(src, dst, swap_send.at[i], swap_recv.at[i], b, partner)
        for i, (src, dst) in enumerate(halves(1 - c))
    ]
    for load in loads:
        load.start()

    bar = pltpu.get_barrier_semaphore()

    def greet(bb, ss):
        pl.semaphore_signal(bar, inc=1, device_id=(bb, ss), device_id_type=MESH)

    def greet_near(i, _):
        db = 1 + i // 4
        greet((b + db) % 4, ((y + i % 4) % 4) * 16 + j16)
        return 0

    lax.fori_loop(0, 12, greet_near, 0)

    def greet_column(i, _):
        greet((b + 1 + i // 3) % 4, q * 4 + (m + 1 + i % 3) % 4)
        return 0

    lax.fori_loop(0, 9, greet_column, 0)

    def greet_group(i, _):
        greet(b, (s + i) % 64)
        return 0

    lax.fori_loop(1, 64, greet_group, 0)

    widened = tok[...].astype(jnp.float32)
    squares = jnp.concatenate([widened * widened] * 4, axis=0)
    row_group = lax.broadcasted_iota(jnp.int32, (128, 128), 0) // 32
    squares = jnp.where(row_group == b, squares, 0.0)
    sq_out[0:1, :] = jnp.sum(squares.T, axis=0, keepdims=True)
    sq_out[1:2, :] = gain[...].astype(jnp.float32)
    my_rows = pl.ds(pl.multiple_of(b * 32, 32), 32)
    sq_in[y * 4 + b] = sq_out[...]

    @pl.when(b == y)
    def _():
        x_in[j16, my_rows, :] = tok[...]

    q32[pl.ds(80 * 32, 128), :] = jnp.zeros((128, 128), jnp.float32)

    row8 = lax.broadcasted_iota(jnp.int32, (8, 128), 0)
    lane8 = lax.broadcasted_iota(jnp.int32, (8, 128), 1)
    place = jnp.zeros((8, 128), jnp.int32)
    for r in range(8):
        place = jnp.where(row8 == r, places[(m % 2) * 8 + r] + m // 2, place)
    angle = place.astype(jnp.float32) * freqs[...]
    cos8 = jnp.cos(angle)
    sin8 = jnp.sin(angle)
    sin8 = jnp.where(lane8 < 64, -sin8, sin8)

    lane = lax.broadcasted_iota(jnp.int32, (16, 128), 1)
    step = lax.broadcasted_iota(jnp.int32, (16, 128), 0) // 8
    which = lane // 16
    for cb in range(2):
        block = s - c + cb
        for bs in range(16):
            rows = pl.ds(cb * 256 + bs * 16, 16)
            dead[rows, :] = jnp.where(lane < lens[bs] - block * 128, 0.0, lowest)
            place = lax.shift_right_arithmetic(lens[bs] + which, 7)
            seen = (lane % 16 == bs) & (which <= step) & (lane < 32) & (place == block)
            dead_extra[rows, :] = jnp.where(seen, 0.0, lowest)

    pl.semaphore_wait(bar, 84)

    def send_rows(i, _):
        yy = (y + 3 - i) % 4

        @pl.when((b != y) | (yy != y))
        def _():
            remote(
                tok, x_in.at[j16, my_rows], s1_send, s1_recv.at[b], y, yy * 16 + j16
            ).start()

        return 0

    lax.fori_loop(0, 4, send_rows, 0)

    def send_squares(i, _):
        remote(
            sq_out, sq_in.at[y * 4 + b], sq_send, sq_recv,
            (b + i // 4) % 4, ((y + i % 4) % 4) * 16 + j16,
        ).start()
        return 0

    lax.fori_loop(1, 16, send_squares, 0)

    swaps[0].start()
    swaps[2].start()

    for i, off in enumerate((0, 1, 3, 2)):
        bb = (b + off) % 4
        piece = x_in.at[j16, pl.ds(pl.multiple_of(bb * 32, 32), 32)]
        if off == 0:
            @pl.when(b != y)
            def _():
                take(s1_recv.at[bb], piece)
        else:
            take(s1_recv.at[bb], piece)

        def send_piece(t, _):
            tt = 7 - t
            xx = (x + gray(tt // 2)) % 4
            zz = (zl + tt) % 2
            cc = jnp.where(tt == 0, 1 - c, c)
            remote(
                piece, piece, x_send, x_direct.at[j16], b, ((y * 4 + xx) * 2 + zz) * 2 + cc
            ).start()
            return 0

        lax.fori_loop(0, 8, send_piece, 0)

    take(sq_recv, sq_in.at[pl.ds(0, 15)])
    a_out[0:1, :] = jnp.sum(sq_in[:, 0:1, :], axis=0)
    a_out[1:2, :] = sq_in[b * 4 + b][1:2, :]
    a_in[j16] = a_out[...]

    def send_stats(i, _):
        remote(
            a_out, a_in.at[j16], a_send, a_recv, b, y * 16 + (j16 + i) % 16
        ).start()
        return 0

    lax.fori_loop(1, 16, send_stats, 0)

    def forward_block(t, _):
        xx = (x + gray(t // 2)) % 4
        zz = (zl + t) % 2
        jj = (xx * 2 + zz) * 2 + c
        block = x_in.at[jj]
        take(x_direct.at[jj], block)
        remote(block, block, xf_send, x_fwd, b, partner).start()
        return 0

    lax.fori_loop(1, 8, forward_block, 0)
    jp = j16 + 1 - 2 * c
    take(x_direct.at[jp], x_in.at[jp])
    take(x_fwd, x_in.at[pl.ds(0, 7)])
    take(a_recv, a_in.at[pl.ds(0, 15)])

    totals = jnp.sum(a_in[:, 0:1, :], axis=0)
    inverse = lax.rsqrt(totals / D + epsilon)
    inverse = jnp.broadcast_to(inverse, (128, 128)).T
    for j in range(16):
        xn[:, j * 128 : (j + 1) * 128] = (
            x_in[j].astype(jnp.float32) * inverse * a_in[j][1:2, :]
        ).astype(jnp.bfloat16)
    loads[0].wait()
    over = (((1,), (1,)), ((), ()))
    product = lax.dot_general(xn[...], wq[...], over, preferred_element_type=jnp.float32)
    product = jnp.concatenate([product, jnp.zeros((128, 96), jnp.float32)], axis=1)
    product = pltpu.roll(product, 32 * m, 1)
    part[...] = product.reshape(16, 8, 256)
    p_in[b * 4 + m] = part[b * 4 + m]

    def send_part(i, _):
        bb = (b + gray(3 - i // 4)) % 4
        mm = (m + 3 - i % 4) % 4
        remote(
            part.at[bb * 4 + mm], p_in.at[b * 4 + m], p_send, p_recv, bb, q * 4 + mm
        ).start()
        return 0

    lax.fori_loop(0, 15, send_part, 0)
    swaps[1].start()
    take(p_recv, p_in.at[pl.ds(0, 15)])

    sums = [p_in[mm] + p_in[4 + mm] + p_in[8 + mm] + p_in[12 + mm] for mm in range(4)]
    for j in range(5):
        head = None
        if j < 4:
            head = sums[j][:, :128]
        if j > 0:
            upper = sums[j - 1][:, 128:]
            head = upper if head is None else head + upper
        head = head.astype(jnp.bfloat16).astype(jnp.float32)
        turned = head * cos8 + pltpu.roll(head, 64, 1) * sin8
        q_out[j] = jnp.where(q * 5 + j < H + KVH, turned, head).astype(jnp.bfloat16)
    g_in[s] = q_out[...]

    def chip_at(t):
        yy = (y + gray(t // 8)) % 4
        xx = (x + gray((t // 2) % 4)) % 4
        zz = (zl + t) % 2
        return ((yy * 4 + xx) * 2 + zz) * 2

    def send_heads(t, _):
        tt = 31 - t
        cc = jnp.where(tt == 0, 1 - c, c)
        remote(q_out, g_in.at[s], g_send, g_direct.at[s], b, chip_at(tt) + cc).start()
        return 0

    lax.fori_loop(0, 32, send_heads, 0)

    def forward_heads(t, _):
        ss = chip_at(t) + c
        block = g_in.at[ss]
        take(g_direct.at[ss], block)
        remote(block, block, gf_send, g_fwd, b, partner).start()
        return 0

    lax.fori_loop(1, 32, forward_heads, 0)
    take(g_direct.at[partner], g_in.at[partner])
    take(g_fwd, g_in.at[pl.ds(0, 31)])

    def spread(qq, _):
        for mm in range(4):
            block = g_in[qq * 4 + mm].astype(jnp.float32)
            for j in range(5):
                at = pl.multiple_of((qq * 5 + j) * 32 + mm * 8, 8)
                q32[pl.ds(at, 8), :] = block[j]
        return 0

    lax.fori_loop(0, 16, spread, 0)

    loads[1].wait()
    loads[2].wait()
    swaps[0].wait_recv()
    swaps[1].wait_recv()
    scale = 1.0 / math.sqrt(HD)

    def kv(i):
        return 4 * c + (s // 8 + i) % 4

    def columns_of(i):
        return pl.ds(pl.multiple_of(((s // 8 + i) % 4) * 128, 128), 128)

    queries = {}

    def fetch(i):
        pieces = []
        for bs in range(16):
            for t in range(2):
                pieces.append(q32[pl.ds(kv(i) * 256 + t * 16 + bs, 8, stride=32), :])
        queries[i] = jnp.concatenate(pieces, axis=0).astype(jnp.bfloat16)
        at = pl.multiple_of((H + kv(i)) * 32, 32)
        raw_extra[i % 2] = lax.dot_general(
            queries[i], q32[pl.ds(at, 128), :].astype(jnp.bfloat16), over,
            preferred_element_type=jnp.float32,
        )

    def score(i, hb, cb):
        for bs in range(hb * 8, hb * 8 + 8):
            raw[i % 2, pl.ds(cb * 256 + bs * 16, 16), :] = lax.dot_general(
                queries[i][bs * 16 : bs * 16 + 16], kc[cb, bs, :, columns_of(i)], over,
                preferred_element_type=jnp.float32,
            )

    def weigh(i, hb, cb):
        rows = pl.ds(cb * 256 + hb * 128, 128)
        scores = raw[i % 2, rows, :] * scale + dead[rows, :]
        extra = raw_extra[i % 2, pl.ds(hb * 128, 128), :] * scale + dead_extra[rows, :]
        peak = jnp.max(jnp.maximum(scores, extra), axis=1, keepdims=True)
        peak = jnp.maximum(peak, floor)
        weights = jnp.exp(scores - peak)
        weights_extra = jnp.exp(extra - peak)
        wts[rows, :] = weights.astype(jnp.bfloat16)
        wts_extra[rows, :] = weights_extra.astype(jnp.bfloat16)
        total = jnp.sum(weights + weights_extra, axis=1, keepdims=True)
        peaks[cb, 0] = jnp.broadcast_to(peak, (128, 128))
        peaks[cb, 1] = jnp.broadcast_to(total, (128, 128))

    def gather_values(i, hb, cb):
        rows = pl.ds(cb * 256 + hb * 128, 128)
        at = pl.multiple_of((H + KVH + kv(i)) * 32, 32)
        sums[cb] = jnp.dot(
            wts_extra[rows, :], q32[pl.ds(at, 128), :].astype(jnp.bfloat16),
            preferred_element_type=jnp.float32,
        )
        for bs in range(8):
            own[cb, pl.ds(bs * 16, 16), :] = jnp.dot(
                wts[pl.ds(cb * 256 + hb * 128 + bs * 16, 16), :],
                vc[cb, hb * 8 + bs, :, columns_of(i)],
                preferred_element_type=jnp.float32,
            )

    stats = {}

    def join(i, hb):
        first, second = peaks[0, 0], peaks[1, 0]
        peak = jnp.maximum(first, second)
        first = jnp.exp(first - peak)
        second = jnp.exp(second - peak)
        total = first * peaks[0, 1] + second * peaks[1, 1]
        summed = first * (own[0] + sums[0]) + second * (own[1] + sums[1])
        if hb == 0:
            stats[i] = jnp.zeros((8, 128), jnp.float32)
        for bs in range(8):
            for t in range(2):
                at = bs * 16 + t * 8
                tb = t * 16 + hb * 8 + bs
                o32[i % 2, pl.ds(tb, 8, stride=32), :] = summed[at : at + 8]
                stats[i] = jnp.where(lane8 == tb, total[at : at + 8], stats[i])
                stats[i] = jnp.where(lane8 == 32 + tb, peak[at : at + 8], stats[i])

    def post(i):
        k = kv(i)
        for g in range(8):
            o_out[k * 8 + g] = o32[i % 2, g * 32 : g * 32 + 32, :].astype(jnp.bfloat16)
            st_out[k * 8 + g] = stats[i][g : g + 1]
        for u in range(8):
            h = k * 8 + (s % 8) ^ u

            def send(recv, st_recv):
                remote(o_out.at[h], o_in.at[chip], o_send, recv, b, h).start()
                remote(st_out.at[h], st_in.at[chip], st_send, st_recv, b, h).start()

            if i == 0 and u < 2:
                @pl.when(half != c)
                def _():
                    send(o_recv, st_recv)

                if u == 1:
                    @pl.when(half == c)
                    def _():
                        send(pair_recv.at[0], pair_recv.at[1])
                else:
                    @pl.when(half == c)
                    def _():
                        o_in[chip] = o_out[h]
                        st_in[chip] = st_out[h]
            else:
                send(o_recv, st_recv)

    groups = [(hb, cb) for hb in range(2) for cb in range(2)]
    fetch(0)
    for hb, cb in groups:
        score(0, hb, cb)
    for i in range(4):
        if i < 3:
            fetch(i + 1)
        for hb, cb in groups:
            if i < 3:
                score(i + 1, hb, cb)
            weigh(i, hb, cb)
            gather_values(i, hb, cb)
            if cb == 1:
                join(i, hb)
        post(i)

    take(st_recv, st_in.at[pl.ds(0, 31)])

    @pl.when(half != c)
    def _():
        take(pair_recv.at[1], st_in.at[0])

    peak = st_in[0]
    for i in range(1, 32):
        peak = jnp.maximum(peak, st_in[i])
    total = jnp.zeros((1, 128), jnp.float32)
    lane1 = lax.broadcasted_iota(jnp.int32, (1, 128), 1)
    for i in range(32):
        row = st_in[i]
        factor = jnp.where((lane1 >= 32) & (lane1 < 64), jnp.exp(row - peak), 0.0)
        fac[i : i + 1, :] = factor
        total = total + factor * pltpu.roll(row, 32, 1)
    fac[32:33, :] = total
    fac[33:128, :] = jnp.zeros((95, 128), jnp.float32)
    factors = fac[...].T[32:64, :]
    take(o_recv, o_in.at[pl.ds(0, 31)])

    @pl.when(half != c)
    def _():
        take(pair_recv.at[0], o_in.at[0])

    summed = jnp.zeros((32, 128), jnp.float32)
    for i in range(32):
        summed = summed + factors[:, i : i + 1] * o_in[i].astype(jnp.float32)
    att[c] = (summed / factors[:, 32:33]).astype(jnp.bfloat16)

    swap = remote(att.at[c], att.at[c], att_send, att_recv, b, partner)
    swap.start()
    loads[3].wait()
    swaps[2].wait_recv()
    swap.wait()
    attended = jnp.concatenate([att[0], att[1]], axis=1)
    for i in range(8):
        chunk = (i + s // 4 + 1) % 8
        cols = pl.ds(pl.multiple_of(chunk * 512, 512), 512)
        weights = jnp.concatenate([wo[0, :, cols], wo[1, :, cols]], axis=0)
        values = jnp.dot(attended, weights, preferred_element_type=jnp.float32)
        for u in range(4):
            y_out[chunk * 4 + u] = values[:, u * 128 : (u + 1) * 128].astype(jnp.bfloat16)
        for u in range(4):
            d = c * 32 + chunk * 4 + m ^ u
            mine = y_out.at[chunk * 4 + m ^ u]

            def send_mixed(recv):
                remote(mine, y_in.at[chip], y_send, recv, b, d).start()

            if i == 7 and u < 2:
                @pl.when(half != c)
                def _():
                    send_mixed(y_recv)

                if u == 1:
                    @pl.when(half == c)
                    def _():
                        send_mixed(pair_recv.at[2])
                else:
                    @pl.when(half == c)
                    def _():
                        y_in[chip] = y_out[chunk * 4 + m]
            else:
                send_mixed(y_recv)

    take(y_recv, y_in.at[pl.ds(0, 31)])

    @pl.when(half != c)
    def _():
        take(pair_recv.at[2], y_in.at[0])

    added = jnp.zeros((32, 128), jnp.float32)
    for i in range(32):
        added = added + y_in[i].astype(jnp.float32)
    out[...] = added

    @pl.when(b != y)
    def _():
        take(s1_send, x_in.at[0])

    @pl.when(b == y)
    def _():
        take(s1_send, x_in.at[0, pl.ds(0, 96)])

    take(sq_send, sq_in.at[pl.ds(0, 15)])
    take(x_send, x_in.at[pl.ds(0, 8)])
    take(xf_send, x_in.at[pl.ds(0, 7)])
    take(a_send, a_in.at[pl.ds(0, 15)])
    take(p_send, p_in.at[pl.ds(0, 15)])
    take(g_send, g_in.at[pl.ds(0, 32)])
    take(gf_send, g_in.at[pl.ds(0, 31)])
    for swap in swaps:
        swap.wait_send()

    @pl.when(half == c)
    def _():
        take(o_send, o_in.at[pl.ds(0, 31)])
        take(st_send, st_in.at[pl.ds(0, 31)])
        take(y_send, y_in.at[pl.ds(0, 31)])

    @pl.when(half != c)
    def _():
        take(o_send, o_in)
        take(st_send, st_in)
        take(y_send, y_in)


def shards(tokens, norm_gain, w_qkv, w_out, cache_keys, cache_values, lengths, positions):
    seqs = tokens.shape[1]
    local_width = tokens.shape[2]
    rows = 2 * seqs
    freqs = rope_base ** (-(np.arange(HD // 2, dtype=np.float64) * 2.0) / HD)
    freqs = np.concatenate([freqs, freqs]).astype(np.float32).reshape(1, HD)
    f32, bf16 = jnp.float32, jnp.bfloat16
    vmem, dma = pltpu.VMEM, pltpu.SemaphoreType.DMA
    whole = pl.BlockSpec(memory_space=pltpu.VMEM)
    hbm = pl.BlockSpec(memory_space=pl.ANY)
    out = pl.pallas_call(
        kernel,
        out_shape=jax.ShapeDtypeStruct((rows, local_width), f32),
        in_specs=[whole] * 3 + [pl.BlockSpec(memory_space=pltpu.SMEM)] * 2 + [hbm] * 4,
        out_specs=whole,
        scratch_shapes=[
            vmem(w_qkv.shape[::-1], bf16),
            vmem((2, 128, 4096), bf16),
            vmem((2, 16, 128, 512), bf16),
            vmem((2, 16, 128, 512), bf16),
            vmem((2, 128), f32),
            vmem((16, 2, 128), f32),
            vmem((16, 128, 128), bf16),
            vmem((2, 128), f32),
            vmem((16, 2, 128), f32),
            vmem((128, 2048), bf16),
            vmem((16, 8, 256), f32),
            vmem((16, 8, 256), f32),
            vmem((5, 8, 128), bf16),
            vmem((64, 5, 8, 128), bf16),
            vmem((84 * 32, 128), f32),
            vmem((512, 128), f32),
            vmem((512, 128), f32),
            vmem((2, 512, 128), f32),
            vmem((2, 256, 128), f32),
            vmem((512, 128), bf16),
            vmem((512, 128), bf16),
            vmem((2, 2, 128, 128), f32),
            vmem((2, 128, 128), f32),
            vmem((2, 128, 128), f32),
            vmem((2, 256, 128), f32),
            vmem((64, 32, 128), bf16),
            vmem((64, 1, 128), f32),
            vmem((32, 32, 128), bf16),
            vmem((32, 1, 128), f32),
            vmem((128, 128), f32),
            vmem((2, 32, 128), bf16),
            vmem((32, 32, 128), bf16),
            vmem((32, 32, 128), bf16),
            dma((4,)), dma((3,)), dma((3,)),
            dma, dma((4,)), dma, dma, dma, dma((16,)), dma, dma, dma, dma,
            dma, dma, dma, dma((64,)), dma, dma,
            dma, dma, dma, dma, dma((3,)), dma, dma, dma, dma,
        ],
        compiler_params=pltpu.CompilerParams(
            collective_id=0, has_side_effects=True, vmem_limit_bytes=60 * 1024 * 1024
        ),
        name="layer",
    )(
        tokens.reshape(rows, local_width), norm_gain.reshape(1, local_width), freqs, lengths, positions,
        w_qkv.T, w_out, cache_keys, cache_values,
    )
    return (tokens.astype(f32) + out.reshape(2, seqs, local_width)).astype(bf16)


def solution(mesh):
    return jax.shard_map(
        shards,
        mesh=mesh,
        in_specs=(
            P(None, "batch", "seq"),
            P("seq"),
            P("batch", "seq"),
            P("seq", None),
            P("batch", "seq", None),
            P("batch", "seq", None),
            P("batch"),
            P("batch"),
        ),
        out_specs=P(None, "batch", "seq"),
        check_vma=False,
    )
```

time: 89.3 us -> 59.4 us (0.67)
  Pallas kernels: 83.3 us -> 57.9 us
  local copies, waits for them, and re-layouts: 3.48 us -> 0.01 us
  other arithmetic: 2.23 us -> 1.32 us
    pallas_call x1, Pallas kernels: 83.3 us -> 57.9 us  [shards(): pl.pallas_call(kernel, out_shape=jax.ShapeDtypeStruct((rows, local_width)...]
    unnamed x2, local copies, waits for them, and re-layouts: 3.48 us -> 0.01 us
where the time goes in v2:
time: 59.4 us; the launch traced here: 59.2 us
  Pallas kernels  57.9 us (97%)
  other arithmetic  1.32 us (2%)
    pallas_call x1, Pallas kernels, shards(): pl.pallas_call(kernel, out_shape=jax.ShapeDtypeStruct((rows, local_width)...  57.9 us
    convert_element_type x1, other arithmetic, shards(): return (tokens.astype(f32) + out.reshape(2, seqs, local_width)).astype(bf16)  1.32 us

profile of v2, /device:TPU:1, one launch (start us, length us, event | category | flops | bytes accessed | tf_op | source)
XLA Modules:
  0.0 59.2 jit_solution(5957662835338739255)
XLA Ops:
  0.0 0.0 copy-start
  0.0 57.9 %layer.1 = f32[32,128]{1,0:T(8,128)} custom-call(bf16[32,128]{1,0:T(8,128)(2,1)} %bitcast.6, bf16[1,128]{1,0:T(2,128)(2,1)} %bitcast.7, f32[1,128]{1,0:T(1,128)} %constant.2.clone.freqs, s32[16]{0:T(128)} %lens.1, s32[16]{0:T(128)} %places.1, bf16[160,2048]{1,0:T(8,128)(2,1)} %bitcast.4, bf16[128,8192]{1,0:T(8,128)(2,1)} %wo_hbm.1, ...), custom_call_target="tpu_custom_call" | custom-call | tf_op jit(solution)/shard_map/layer/pallas_call | solution.py:537
  57.9 0.0 copy-done
  57.9 1.3 %add_convert_fusion = bf16[2,16,128]{2,1,0:T(8,128)(2,1)} fusion(f32[2,16,128]{2,1,0:T(8,128)} %bitcast.5, bf16[2,16,128]{2,1,0:T(8,128)(2,1)S(1)} %copy-done), kind=kLoop, calls=%fused_computation | loop fusion | flops 12288 | bytes 32768 | tf_op jit(solution)/shard_map/convert_element_type | solution.py:589
Async XLA Ops:
  0.0 57.9 %copy-start = (bf16[2,16,128]{2,1,0:T(8,128)(2,1)S(1)}, bf16[2,16,128]{2,1,0:T(8,128)(2,1)}, u32[]{:S(2)}) copy-start(bf16[2,16,128]{2,1,0:T(8,128)(2,1)} %param.9) | copy-start | bytes 24580

commit v3 on v2

--- a/solution.py
+++ b/solution.py
@@ -30,11 +30,10 @@
     sq_out, sq_in, x_in, a_out, a_in, xn,
     part, p_in, q_out, g_in, q32,
     dead, dead_extra, raw, raw_extra, wts, wts_extra, peaks, sums, own,
-    o32, o_out, st_out, o_in, st_in, fac, att, y_out, y_in,
+    o32, o_out, st_out, o_in, st_in, fac, y_out, y_in,
     hbm_sem, swap_send, swap_recv,
     s1_send, s1_recv, sq_send, sq_recv, x_send, x_direct, xf_send, x_fwd, a_send, a_recv,
-    p_send, p_recv, g_send, g_direct, gf_send, g_fwd,
-    o_send, o_recv, st_send, st_recv, pair_recv, att_send, att_recv, y_send, y_recv,
+    p_send, p_recv, g_send, g_recv, o_send, o_recv, st_send, st_recv, y_send, y_recv,
 ):
     b = lax.axis_index("batch")
     s = lax.axis_index("seq")
@@ -46,7 +45,6 @@
     q = s // 4
     j16 = s % 16
     partner = s + 1 - 2 * c
-    half = s // 32
     chip = s // 2
 
     def remote(src, dst, send, recv, bb, ss):
@@ -59,12 +57,10 @@
         pltpu.make_async_copy(ref, ref, sem).wait()
 
     def halves(cc):
-        cols = pl.ds(pl.multiple_of(cc * 512, 512), 512)
-        wide = pl.ds(pl.multiple_of(cc * 4096, 4096), 4096)
         return (
-            (k_hbm.at[:, :, cols], kc.at[c]),
-            (v_hbm.at[:, :, cols], vc.at[c]),
-            (wo_hbm.at[:, wide], wo.at[c]),
+            (k_hbm.at[pl.ds(cc * 8, 8)], kc.at[c]),
+            (v_hbm.at[pl.ds(cc * 8, 8)], vc.at[c]),
+            (wo_hbm, wo.at[c]),
         )
 
     loads = [
@@ -115,7 +111,7 @@
     def _():
         x_in[j16, my_rows, :] = tok[...]
 
-    q32[pl.ds(80 * 32, 128), :] = jnp.zeros((128, 128), jnp.float32)
+    q32[pl.ds(80 * 16, 128), :] = jnp.zeros((128, 128), jnp.float32)
 
     row8 = lax.broadcasted_iota(jnp.int32, (8, 128), 0)
     lane8 = lax.broadcasted_iota(jnp.int32, (8, 128), 1)
@@ -129,14 +125,15 @@
 
     lane = lax.broadcasted_iota(jnp.int32, (16, 128), 1)
     step = lax.broadcasted_iota(jnp.int32, (16, 128), 0) // 8
-    which = lane // 16
+    which = lane // 8
     for cb in range(2):
         block = s - c + cb
-        for bs in range(16):
-            rows = pl.ds(cb * 256 + bs * 16, 16)
-            dead[rows, :] = jnp.where(lane < lens[bs] - block * 128, 0.0, lowest)
-            place = lax.shift_right_arithmetic(lens[bs] + which, 7)
-            seen = (lane % 16 == bs) & (which <= step) & (lane < 32) & (place == block)
+        for bs in range(8):
+            length = lens[c * 8 + bs]
+            rows = pl.ds(cb * 128 + bs * 16, 16)
+            dead[rows, :] = jnp.where(lane < length - block * 128, 0.0, lowest)
+            place = lax.shift_right_arithmetic(length + which, 7)
+            seen = (lane % 8 == bs) & (which <= step) & (lane < 16) & (place == block)
             dead_extra[rows, :] = jnp.where(seen, 0.0, lowest)
 
     pl.semaphore_wait(bar, 84)
@@ -164,7 +161,6 @@
     lax.fori_loop(1, 16, send_squares, 0)
 
     swaps[0].start()
-    swaps[2].start()
 
     for i, off in enumerate((0, 1, 3, 2)):
         bb = (b + off) % 4
@@ -241,6 +237,7 @@
 
     lax.fori_loop(0, 15, send_part, 0)
     swaps[1].start()
+    swaps[2].start()
     take(p_recv, p_in.at[pl.ds(0, 15)])
 
     sums = [p_in[mm] + p_in[4 + mm] + p_in[8 + mm] + p_in[12 + mm] for mm in range(4)]
@@ -254,7 +251,7 @@
         head = head.astype(jnp.bfloat16).astype(jnp.float32)
         turned = head * cos8 + pltpu.roll(head, 64, 1) * sin8
         q_out[j] = jnp.where(q * 5 + j < H + KVH, turned, head).astype(jnp.bfloat16)
-    g_in[s] = q_out[...]
+    g_in[chip] = q_out[...]
 
     def chip_at(t):
         yy = (y + gray(t // 8)) % 4
@@ -263,29 +260,17 @@
         return ((yy * 4 + xx) * 2 + zz) * 2
 
     def send_heads(t, _):
-        tt = 31 - t
-        cc = jnp.where(tt == 0, 1 - c, c)
-        remote(q_out, g_in.at[s], g_send, g_direct.at[s], b, chip_at(tt) + cc).start()
-        return 0
-
-    lax.fori_loop(0, 32, send_heads, 0)
-
-    def forward_heads(t, _):
-        ss = chip_at(t) + c
-        block = g_in.at[ss]
-        take(g_direct.at[ss], block)
-        remote(block, block, gf_send, g_fwd, b, partner).start()
-        return 0
-
-    lax.fori_loop(1, 32, forward_heads, 0)
-    take(g_direct.at[partner], g_in.at[partner])
-    take(g_fwd, g_in.at[pl.ds(0, 31)])
+        remote(q_out, g_in.at[chip], g_send, g_recv, b, chip_at(31 - t) + c).start()
+        return 0
+
+    lax.fori_loop(0, 31, send_heads, 0)
+    take(g_recv, g_in.at[pl.ds(0, 31)])
 
     def spread(qq, _):
-        for mm in range(4):
-            block = g_in[qq * 4 + mm].astype(jnp.float32)
+        for t in range(2):
+            block = g_in[qq * 2 + t].astype(jnp.float32)
             for j in range(5):
-                at = pl.multiple_of((qq * 5 + j) * 32 + mm * 8, 8)
+                at = pl.multiple_of((qq * 5 + j) * 16 + t * 8, 8)
                 q32[pl.ds(at, 8), :] = block[j]
         return 0
 
@@ -297,37 +282,38 @@
     swaps[1].wait_recv()
     scale = 1.0 / math.sqrt(HD)
 
-    def kv(i):
-        return 4 * c + (s // 8 + i) % 4
-
-    def columns_of(i):
-        return pl.ds(pl.multiple_of(((s // 8 + i) % 4) * 128, 128), 128)
+    def kv(i, kh):
+        return (s // 16 + i) % 4 * 2 + kh
+
+    def columns_of(i, kh):
+        return pl.ds(pl.multiple_of(kv(i, kh) * 128, 128), 128)
 
     queries = {}
 
     def fetch(i):
-        pieces = []
-        for bs in range(16):
-            for t in range(2):
-                pieces.append(q32[pl.ds(kv(i) * 256 + t * 16 + bs, 8, stride=32), :])
-        queries[i] = jnp.concatenate(pieces, axis=0).astype(jnp.bfloat16)
-        at = pl.multiple_of((H + kv(i)) * 32, 32)
-        raw_extra[i % 2] = lax.dot_general(
-            queries[i], q32[pl.ds(at, 128), :].astype(jnp.bfloat16), over,
-            preferred_element_type=jnp.float32,
-        )
-
-    def score(i, hb, cb):
-        for bs in range(hb * 8, hb * 8 + 8):
-            raw[i % 2, pl.ds(cb * 256 + bs * 16, 16), :] = lax.dot_general(
-                queries[i][bs * 16 : bs * 16 + 16], kc[cb, bs, :, columns_of(i)], over,
+        for kh in range(2):
+            pieces = []
+            for bs in range(8):
+                for t in range(2):
+                    pieces.append(q32[pl.ds(kv(i, kh) * 128 + t * 8 + bs, 8, stride=16), :])
+            queries[i, kh] = jnp.concatenate(pieces, axis=0).astype(jnp.bfloat16)
+            at = pl.multiple_of((H + kv(i, kh)) * 16, 16)
+            raw_extra[i % 2, pl.ds(kh * 128, 128), :] = lax.dot_general(
+                queries[i, kh], q32[pl.ds(at, 128), :].astype(jnp.bfloat16), over,
                 preferred_element_type=jnp.float32,
             )
 
+    def score(i, kh, cb):
+        for bs in range(8):
+            raw[i % 2, pl.ds(cb * 256 + kh * 128 + bs * 16, 16), :] = lax.dot_general(
+                queries[i, kh][bs * 16 : bs * 16 + 16], kc[cb, bs, :, columns_of(i, kh)], over,
+                preferred_element_type=jnp.float32,
+            )
+
     def weigh(i, hb, cb):
         rows = pl.ds(cb * 256 + hb * 128, 128)
-        scores = raw[i % 2, rows, :] * scale + dead[rows, :]
-        extra = raw_extra[i % 2, pl.ds(hb * 128, 128), :] * scale + dead_extra[rows, :]
+        scores = raw[i % 2, rows, :] * scale + dead[pl.ds(cb * 128, 128), :]
+        extra = raw_extra[i % 2, pl.ds(hb * 128, 128), :] * scale + dead_extra[pl.ds(cb * 128, 128), :]
         peak = jnp.max(jnp.maximum(scores, extra), axis=1, keepdims=True)
         peak = jnp.maximum(peak, floor)
         weights = jnp.exp(scores - peak)
@@ -340,7 +326,7 @@
 
     def gather_values(i, hb, cb):
         rows = pl.ds(cb * 256 + hb * 128, 128)
-        at = pl.multiple_of((H + KVH + kv(i)) * 32, 32)
+        at = pl.multiple_of((H + KVH + kv(i, hb)) * 16, 16)
         sums[cb] = jnp.dot(
             wts_extra[rows, :], q32[pl.ds(at, 128), :].astype(jnp.bfloat16),
             preferred_element_type=jnp.float32,
@@ -348,7 +334,7 @@
         for bs in range(8):
             own[cb, pl.ds(bs * 16, 16), :] = jnp.dot(
                 wts[pl.ds(cb * 256 + hb * 128 + bs * 16, 16), :],
-                vc[cb, hb * 8 + bs, :, columns_of(i)],
+                vc[cb, bs, :, columns_of(i, hb)],
                 preferred_element_type=jnp.float32,
             )
 
@@ -361,44 +347,33 @@
         second = jnp.exp(second - peak)
         total = first * peaks[0, 1] + second * peaks[1, 1]
         summed = first * (own[0] + sums[0]) + second * (own[1] + sums[1])
-        if hb == 0:
-            stats[i] = jnp.zeros((8, 128), jnp.float32)
+        stat = jnp.zeros((8, 128), jnp.float32)
         for bs in range(8):
             for t in range(2):
                 at = bs * 16 + t * 8
-                tb = t * 16 + hb * 8 + bs
-                o32[i % 2, pl.ds(tb, 8, stride=32), :] = summed[at : at + 8]
-                stats[i] = jnp.where(lane8 == tb, total[at : at + 8], stats[i])
-                stats[i] = jnp.where(lane8 == 32 + tb, peak[at : at + 8], stats[i])
-
-    def post(i):
-        k = kv(i)
-        for g in range(8):
-            o_out[k * 8 + g] = o32[i % 2, g * 32 : g * 32 + 32, :].astype(jnp.bfloat16)
-            st_out[k * 8 + g] = stats[i][g : g + 1]
-        for u in range(8):
-            h = k * 8 + (s % 8) ^ u
-
-            def send(recv, st_recv):
-                remote(o_out.at[h], o_in.at[chip], o_send, recv, b, h).start()
-                remote(st_out.at[h], st_in.at[chip], st_send, st_recv, b, h).start()
-
-            if i == 0 and u < 2:
-                @pl.when(half != c)
-                def _():
-                    send(o_recv, st_recv)
-
-                if u == 1:
-                    @pl.when(half == c)
-                    def _():
-                        send(pair_recv.at[0], pair_recv.at[1])
-                else:
-                    @pl.when(half == c)
-                    def _():
-                        o_in[chip] = o_out[h]
-                        st_in[chip] = st_out[h]
+                tb = t * 8 + bs
+                o32[hb, pl.ds(tb, 8, stride=16), :] = summed[at : at + 8]
+                stat = jnp.where(lane8 == tb, total[at : at + 8], stat)
+                stat = jnp.where(lane8 == 32 + tb, peak[at : at + 8], stat)
+        stats[i, hb] = (stat, pltpu.roll(stat, 16, 1))
+
+    def post(i, hb):
+        for p in range(4):
+            dest = kv(i, hb) * 4 + p
+            o_out[dest] = o32[hb, p * 32 : p * 32 + 32, :].astype(jnp.bfloat16)
+            stat, turned = stats[i, hb]
+            st_out[dest] = stat[2 * p : 2 * p + 1] + turned[2 * p + 1 : 2 * p + 2]
+        for p in range(4):
+            dest = kv(i, hb) * 4 + p
+
+            def send():
+                remote(o_out.at[dest], o_in.at[chip], o_send, o_recv, b, dest * 2 + c).start()
+                remote(st_out.at[dest], st_in.at[chip], st_send, st_recv, b, dest * 2 + c).start()
+
+            if i == 0:
+                pl.when(dest != chip)(send)
             else:
-                send(o_recv, st_recv)
+                send()
 
     groups = [(hb, cb) for hb in range(2) for cb in range(2)]
     fetch(0)
@@ -414,13 +389,10 @@
             gather_values(i, hb, cb)
             if cb == 1:
                 join(i, hb)
-        post(i)
-
+                post(i, hb)
+    o_in[chip] = o_out[chip]
+    st_in[chip] = st_out[chip]
     take(st_recv, st_in.at[pl.ds(0, 31)])
-
-    @pl.when(half != c)
-    def _():
-        take(pair_recv.at[1], st_in.at[0])
 
     peak = st_in[0]
     for i in range(1, 32):
@@ -436,62 +408,33 @@
     fac[33:128, :] = jnp.zeros((95, 128), jnp.float32)
     factors = fac[...].T[32:64, :]
     take(o_recv, o_in.at[pl.ds(0, 31)])
-
-    @pl.when(half != c)
-    def _():
-        take(pair_recv.at[0], o_in.at[0])
-
     summed = jnp.zeros((32, 128), jnp.float32)
     for i in range(32):
         summed = summed + factors[:, i : i + 1] * o_in[i].astype(jnp.float32)
-    att[c] = (summed / factors[:, 32:33]).astype(jnp.bfloat16)
-
-    swap = remote(att.at[c], att.at[c], att_send, att_recv, b, partner)
-    swap.start()
+    attended = summed / factors[:, 32:33]
+    attended = jnp.concatenate([attended[:16], attended[16:]], axis=1).astype(jnp.bfloat16)
+
     loads[3].wait()
     swaps[2].wait_recv()
-    swap.wait()
-    attended = jnp.concatenate([att[0], att[1]], axis=1)
-    for i in range(8):
-        chunk = (i + s // 4 + 1) % 8
+    for i in range(16):
+        chunk = (i + q + 1) % 16
         cols = pl.ds(pl.multiple_of(chunk * 512, 512), 512)
         weights = jnp.concatenate([wo[0, :, cols], wo[1, :, cols]], axis=0)
         values = jnp.dot(attended, weights, preferred_element_type=jnp.float32)
         for u in range(4):
             y_out[chunk * 4 + u] = values[:, u * 128 : (u + 1) * 128].astype(jnp.bfloat16)
         for u in range(4):
-            d = c * 32 + chunk * 4 + m ^ u
-            mine = y_out.at[chunk * 4 + m ^ u]
-
-            def send_mixed(recv):
-                remote(mine, y_in.at[chip], y_send, recv, b, d).start()
-
-            if i == 7 and u < 2:
-                @pl.when(half != c)
-                def _():
-                    send_mixed(y_recv)
-
-                if u == 1:
-                    @pl.when(half == c)
-                    def _():
-                        send_mixed(pair_recv.at[2])
-                else:
-                    @pl.when(half == c)
-                    def _():
-                        y_in[chip] = y_out[chunk * 4 + m]
-            else:
-                send_mixed(y_recv)
-
-    take(y_recv, y_in.at[pl.ds(0, 31)])
-
-    @pl.when(half != c)
-    def _():
-        take(pair_recv.at[2], y_in.at[0])
-
-    added = jnp.zeros((32, 128), jnp.float32)
-    for i in range(32):
-        added = added + y_in[i].astype(jnp.float32)
-    out[...] = added
+            d = chunk * 4 + m ^ u
+            if i < 15 or u > 0:
+                remote(y_out.at[d], y_in.at[c * 32 + chip], y_send, y_recv, b, d).start()
+    y_in[c * 32 + chip] = y_out[s]
+    take(y_recv, y_in.at[pl.ds(0, 63)])
+    for half in range(2):
+        added = jnp.zeros((16, 128), jnp.float32)
+        for i in range(32):
+            added = added + y_in[half * 32 + i].astype(jnp.float32)
+        for t in range(2):
+            out[t * 16 + half * 8 : t * 16 + half * 8 + 8, :] = added[t * 8 : t * 8 + 8]
 
     @pl.when(b != y)
     def _():
@@ -506,22 +449,12 @@
     take(xf_send, x_in.at[pl.ds(0, 7)])
     take(a_send, a_in.at[pl.ds(0, 15)])
     take(p_send, p_in.at[pl.ds(0, 15)])
-    take(g_send, g_in.at[pl.ds(0, 32)])
-    take(gf_send, g_in.at[pl.ds(0, 31)])
+    take(g_send, g_in.at[pl.ds(0, 31)])
     for swap in swaps:
         swap.wait_send()
-
-    @pl.when(half == c)
-    def _():
-        take(o_send, o_in.at[pl.ds(0, 31)])
-        take(st_send, st_in.at[pl.ds(0, 31)])
-        take(y_send, y_in.at[pl.ds(0, 31)])
-
-    @pl.when(half != c)
-    def _():
-        take(o_send, o_in)
-        take(st_send, st_in)
-        take(y_send, y_in)
+    take(o_send, o_in.at[pl.ds(0, 31)])
+    take(st_send, st_in.at[pl.ds(0, 31)])
+    take(y_send, y_in.at[pl.ds(0, 63)])
 
 
 def shards(tokens, norm_gain, w_qkv, w_out, cache_keys, cache_values, lengths, positions):
@@ -541,9 +474,9 @@
         out_specs=whole,
         scratch_shapes=[
             vmem(w_qkv.shape[::-1], bf16),
-            vmem((2, 128, 4096), bf16),
-            vmem((2, 16, 128, 512), bf16),
-            vmem((2, 16, 128, 512), bf16),
+            vmem((2, *w_out.shape), bf16),
+            vmem((2, 8, 128, 1024), bf16),
+            vmem((2, 8, 128, 1024), bf16),
             vmem((2, 128), f32),
             vmem((16, 2, 128), f32),
             vmem((16, 128, 128), bf16),
@@ -553,10 +486,10 @@
             vmem((16, 8, 256), f32),
             vmem((16, 8, 256), f32),
             vmem((5, 8, 128), bf16),
-            vmem((64, 5, 8, 128), bf16),
-            vmem((84 * 32, 128), f32),
-            vmem((512, 128), f32),
-            vmem((512, 128), f32),
+            vmem((32, 5, 8, 128), bf16),
+            vmem((88 * 16, 128), f32),
+            vmem((256, 128), f32),
+            vmem((256, 128), f32),
             vmem((2, 512, 128), f32),
             vmem((2, 256, 128), f32),
             vmem((512, 128), bf16),
@@ -564,19 +497,17 @@
             vmem((2, 2, 128, 128), f32),
             vmem((2, 128, 128), f32),
             vmem((2, 128, 128), f32),
-            vmem((2, 256, 128), f32),
-            vmem((64, 32, 128), bf16),
-            vmem((64, 1, 128), f32),
+            vmem((2, 128, 128), f32),
+            vmem((32, 32, 128), bf16),
+            vmem((32, 1, 128), f32),
             vmem((32, 32, 128), bf16),
             vmem((32, 1, 128), f32),
             vmem((128, 128), f32),
-            vmem((2, 32, 128), bf16),
-            vmem((32, 32, 128), bf16),
-            vmem((32, 32, 128), bf16),
+            vmem((64, 16, 128), bf16),
+            vmem((64, 16, 128), bf16),
             dma((4,)), dma((3,)), dma((3,)),
             dma, dma((4,)), dma, dma, dma, dma((16,)), dma, dma, dma, dma,
-            dma, dma, dma, dma((64,)), dma, dma,
-            dma, dma, dma, dma, dma((3,)), dma, dma, dma, dma,
+            dma, dma, dma, dma, dma, dma, dma, dma, dma, dma,
         ],
         compiler_params=pltpu.CompilerParams(
             collective_id=0, has_side_effects=True, vmem_limit_bytes=60 * 1024 * 1024

time: 59.4 us -> 55.6 us (0.936)
  Pallas kernels: 57.9 us -> 54 us
    pallas_call x1, Pallas kernels: 57.9 us -> 54 us  [shards(): pl.pallas_call(kernel, out_shape=jax.ShapeDtypeStruct((rows, local_width)...]
where the time goes in v3:
time: 55.6 us; the launch traced here: 55.4 us
  Pallas kernels  54 us (97%)
  other arithmetic  1.32 us (2%)
    pallas_call x1, Pallas kernels, shards(): pl.pallas_call(kernel, out_shape=jax.ShapeDtypeStruct((rows, local_width)...  54 us
    convert_element_type x1, other arithmetic, shards(): return (tokens.astype(f32) + out.reshape(2, seqs, local_width)).astype(bf16)  1.32 us

profile of v3, /device:TPU:1, one launch (start us, length us, event | category | flops | bytes accessed | tf_op | source)
XLA Modules:
  0.0 55.4 jit_solution(18005476389691742245)
XLA Ops:
  0.0 0.0 copy-start
  0.0 54.0 %layer.1 = f32[32,128]{1,0:T(8,128)} custom-call(bf16[32,128]{1,0:T(8,128)(2,1)} %bitcast.6, bf16[1,128]{1,0:T(2,128)(2,1)} %bitcast.7, f32[1,128]{1,0:T(1,128)} %constant.2.clone.freqs, s32[16]{0:T(128)} %lens.1, s32[16]{0:T(128)} %places.1, bf16[160,2048]{1,0:T(8,128)(2,1)} %bitcast.4, bf16[128,8192]{1,0:T(8,128)(2,1)} %wo_hbm.1, ...), custom_call_target="tpu_custom_call" | custom-call | tf_op jit(solution)/shard_map/layer/pallas_call | solution.py:470
  54.1 0.0 copy-done
  54.1 1.3 %add_convert_fusion = bf16[2,16,128]{2,1,0:T(8,128)(2,1)} fusion(f32[2,16,128]{2,1,0:T(8,128)} %bitcast.5, bf16[2,16,128]{2,1,0:T(8,128)(2,1)S(1)} %copy-done), kind=kLoop, calls=%fused_computation | loop fusion | flops 12288 | bytes 32768 | tf_op jit(solution)/shard_map/convert_element_type | solution.py:520
Async XLA Ops:
  0.0 54.1 %copy-start = (bf16[2,16,128]{2,1,0:T(8,128)(2,1)S(1)}, bf16[2,16,128]{2,1,0:T(8,128)(2,1)}, u32[]{:S(2)}) copy-start(bf16[2,16,128]{2,1,0:T(8,128)(2,1)} %param.9) | copy-start | bytes 24580

commit v4 on v3

--- a/solution.py
+++ b/solution.py
@@ -80,23 +80,11 @@
         pl.semaphore_signal(bar, inc=1, device_id=(bb, ss), device_id_type=MESH)
 
     def greet_near(i, _):
-        db = 1 + i // 4
-        greet((b + db) % 4, ((y + i % 4) % 4) * 16 + j16)
-        return 0
-
-    lax.fori_loop(0, 12, greet_near, 0)
-
-    def greet_column(i, _):
-        greet((b + 1 + i // 3) % 4, q * 4 + (m + 1 + i % 3) % 4)
-        return 0
-
-    lax.fori_loop(0, 9, greet_column, 0)
-
-    def greet_group(i, _):
-        greet(b, (s + i) % 64)
-        return 0
-
-    lax.fori_loop(1, 64, greet_group, 0)
+        greet((b + i // 4) % 4, ((y + i % 4) % 4) * 16 + j16)
+        greet(b, y * 16 + (j16 + i) % 16)
+        return 0
+
+    lax.fori_loop(1, 16, greet_near, 0)
 
     widened = tok[...].astype(jnp.float32)
     squares = jnp.concatenate([widened * widened] * 4, axis=0)
@@ -136,7 +124,7 @@
             seen = (lane % 8 == bs) & (which <= step) & (lane < 16) & (place == block)
             dead_extra[rows, :] = jnp.where(seen, 0.0, lowest)
 
-    pl.semaphore_wait(bar, 84)
+    pl.semaphore_wait(bar, 30)
 
     def send_rows(i, _):
         yy = (y + 3 - i) % 4
@@ -283,7 +271,7 @@
     scale = 1.0 / math.sqrt(HD)
 
     def kv(i, kh):
-        return (s // 16 + i) % 4 * 2 + kh
+        return (y + gray(3 - i)) % 4 * 2 + kh
 
     def columns_of(i, kh):
         return pl.ds(pl.multiple_of(kv(i, kh) * 128, 128), 128)
@@ -370,7 +358,7 @@
                 remote(o_out.at[dest], o_in.at[chip], o_send, o_recv, b, dest * 2 + c).start()
                 remote(st_out.at[dest], st_in.at[chip], st_send, st_recv, b, dest * 2 + c).start()
 
-            if i == 0:
+            if i == 3:
                 pl.when(dest != chip)(send)
             else:
                 send()
@@ -416,17 +404,28 @@
 
     loads[3].wait()
     swaps[2].wait_recv()
-    for i in range(16):
-        chunk = (i + q + 1) % 16
-        cols = pl.ds(pl.multiple_of(chunk * 512, 512), 512)
+
+    def chunk_at(i):
+        return (y + gray(3 - i // 4)) % 4 * 4 + (x + gray(3 - i % 4)) % 4
+
+    def project(i):
+        cols = pl.ds(pl.multiple_of(chunk_at(i) * 512, 512), 512)
         weights = jnp.concatenate([wo[0, :, cols], wo[1, :, cols]], axis=0)
-        values = jnp.dot(attended, weights, preferred_element_type=jnp.float32)
-        for u in range(4):
-            y_out[chunk * 4 + u] = values[:, u * 128 : (u + 1) * 128].astype(jnp.bfloat16)
-        for u in range(4):
-            d = chunk * 4 + m ^ u
-            if i < 15 or u > 0:
-                remote(y_out.at[d], y_in.at[c * 32 + chip], y_send, y_recv, b, d).start()
+        return jnp.dot(attended, weights, preferred_element_type=jnp.float32)
+
+    ahead = 4
+    values = [project(i) for i in range(ahead)]
+    for i in range(0, 16, ahead):
+        now = values
+        values = [project(j) for j in range(i + ahead, min(16, i + 2 * ahead))]
+        for j in range(ahead):
+            for u in range(4):
+                y_out[chunk_at(i + j) * 4 + u] = now[j][:, u * 128 : (u + 1) * 128].astype(jnp.bfloat16)
+        for j in range(ahead):
+            for u in range(4):
+                d = chunk_at(i + j) * 4 + m ^ u
+                if i + j < 15 or u > 0:
+                    remote(y_out.at[d], y_in.at[c * 32 + chip], y_send, y_recv, b, d).start()
     y_in[c * 32 + chip] = y_out[s]
     take(y_recv, y_in.at[pl.ds(0, 63)])
     for half in range(2):
@@ -469,7 +468,7 @@
     hbm = pl.BlockSpec(memory_space=pl.ANY)
     out = pl.pallas_call(
         kernel,
-        out_shape=jax.ShapeDtypeStruct((rows, local_width), f32),
+        out_shape=pltpu.VMEM((rows, local_width), f32),
         in_specs=[whole] * 3 + [pl.BlockSpec(memory_space=pltpu.SMEM)] * 2 + [hbm] * 4,
         out_specs=whole,
         scratch_shapes=[

time: 55.6 us -> 53.3 us (0.959)
  Pallas kernels: 54 us -> 52.5 us
  other arithmetic: 1.32 us -> 0.6 us
    pallas_call x1, Pallas kernels: 54 us -> 52.5 us  [shards(): pl.pallas_call(kernel, out_shape=pltpu.VMEM((rows, local_width), f32), in...]
    convert_element_type x1, other arithmetic: 1.32 us -> 0.6 us  [shards(): return (tokens.astype(f32) + out.reshape(2, seqs, local_width)).astype(bf16)]
where the time goes in v4:
time: 53.3 us; the launch traced here: 53.2 us
  Pallas kernels  52.5 us (98%)
  other arithmetic  0.6 us (1%)
    pallas_call x1, Pallas kernels, shards(): pl.pallas_call(kernel, out_shape=pltpu.VMEM((rows, local_width), f32), in...  52.5 us

profile of v4, /device:TPU:1, one launch (start us, length us, event | category | flops | bytes accessed | tf_op | source)
XLA Modules:
  0.0 53.2 jit_solution(13156897498887366267)
XLA Ops:
  0.0 0.0 copy-start
  0.0 52.5 %layer.1 = f32[32,128]{1,0:T(8,128)S(1)} custom-call(bf16[32,128]{1,0:T(8,128)(2,1)} %bitcast.6, bf16[1,128]{1,0:T(2,128)(2,1)} %bitcast.7, f32[1,128]{1,0:T(1,128)} %constant.2.clone.freqs, s32[16]{0:T(128)} %lens.1, s32[16]{0:T(128)} %places.1, bf16[160,2048]{1,0:T(8,128)(2,1)} %bitcast.5, bf16[128,8192]{1,0:T(8,128)(2,1)} %wo_hbm.1, ...), custom_call_target="tpu_custom_call" | custom-call | tf_op jit(solution)/shard_map/layer/pallas_call | solution.py:469
  52.6 0.0 copy-done
  52.6 0.6 %add_convert_fusion = bf16[2,16,128]{2,1,0:T(8,128)(2,1)} fusion(f32[2,16,128]{2,1,0:T(8,128)S(1)} %bitcast.4, bf16[2,16,128]{2,1,0:T(8,128)(2,1)S(1)} %copy-done), kind=kLoop, calls=%fused_computation | loop fusion | flops 12288 | bytes 32768 | tf_op jit(solution)/shard_map/convert_element_type | solution.py:519
Async XLA Ops:
  0.0 52.6 %copy-start = (bf16[2,16,128]{2,1,0:T(8,128)(2,1)S(1)}, bf16[2,16,128]{2,1,0:T(8,128)(2,1)}, u32[]{:S(2)}) copy-start(bf16[2,16,128]{2,1,0:T(8,128)(2,1)} %param.9) | copy-start | bytes 24580

commit v5 on v4

--- a/solution.py
+++ b/solution.py
@@ -32,7 +32,7 @@
     dead, dead_extra, raw, raw_extra, wts, wts_extra, peaks, sums, own,
     o32, o_out, st_out, o_in, st_in, fac, y_out, y_in,
     hbm_sem, swap_send, swap_recv,
-    s1_send, s1_recv, sq_send, sq_recv, x_send, x_direct, xf_send, x_fwd, a_send, a_recv,
+    s1_send, s1_recv, sq_send, sq_recv, x_send, x_direct, xl_send, x_last, xf_send, x_fwd, a_send, a_recv,
     p_send, p_recv, g_send, g_recv, o_send, o_recv, st_send, st_recv, y_send, y_recv,
 ):
     b = lax.axis_index("batch")
@@ -170,34 +170,51 @@
             ).start()
             return 0
 
-        lax.fori_loop(0, 8, send_piece, 0)
-
-    take(sq_recv, sq_in.at[pl.ds(0, 15)])
-    a_out[0:1, :] = jnp.sum(sq_in[:, 0:1, :], axis=0)
-    a_out[1:2, :] = sq_in[b * 4 + b][1:2, :]
-    a_in[j16] = a_out[...]
-
-    def send_stats(i, _):
-        remote(
-            a_out, a_in.at[j16], a_send, a_recv, b, y * 16 + (j16 + i) % 16
-        ).start()
-        return 0
-
-    lax.fori_loop(1, 16, send_stats, 0)
+        def send_last(t, _):
+            tt = 15 - t
+            xx = (x + gray(tt // 4)) % 4
+            zz = (zl + tt // 2) % 2
+            cc = (c + tt) % 2
+            remote(
+                piece, piece, xl_send, x_last, b, ((y * 4 + xx) * 2 + zz) * 2 + cc
+            ).start()
+            return 0
+
+        if off == 2:
+            lax.fori_loop(0, 15, send_last, 0)
+        else:
+            lax.fori_loop(0, 8, send_piece, 0)
+        if off == 3:
+            take(sq_recv, sq_in.at[pl.ds(0, 15)])
+            a_out[0:1, :] = jnp.sum(sq_in[:, 0:1, :], axis=0)
+            a_out[1:2, :] = sq_in[b * 4 + b][1:2, :]
+            a_in[j16] = a_out[...]
+
+            def send_stats(i, _):
+                remote(
+                    a_out, a_in.at[j16], a_send, a_recv, b, y * 16 + (j16 + i) % 16
+                ).start()
+                return 0
+
+            lax.fori_loop(1, 16, send_stats, 0)
+
+    early = o_out.at[pl.ds(0, 3)]
 
     def forward_block(t, _):
         xx = (x + gray(t // 2)) % 4
         zz = (zl + t) % 2
         jj = (xx * 2 + zz) * 2 + c
-        block = x_in.at[jj]
-        take(x_direct.at[jj], block)
-        remote(block, block, xf_send, x_fwd, b, partner).start()
+        take(x_direct.at[jj], early)
+        for off in (0, 1, 3):
+            bb = (b + off) % 4
+            piece = x_in.at[jj, pl.ds(pl.multiple_of(bb * 32, 32), 32)]
+            remote(piece, piece, xf_send, x_fwd, b, partner).start()
         return 0
 
     lax.fori_loop(1, 8, forward_block, 0)
-    jp = j16 + 1 - 2 * c
-    take(x_direct.at[jp], x_in.at[jp])
-    take(x_fwd, x_in.at[pl.ds(0, 7)])
+    take(x_direct.at[j16 + 1 - 2 * c], early)
+    take(x_fwd, o_out.at[pl.ds(0, 21)])
+    take(x_last, o_out.at[pl.ds(0, 15)])
     take(a_recv, a_in.at[pl.ds(0, 15)])
 
     totals = jnp.sum(a_in[:, 0:1, :], axis=0)
@@ -271,7 +288,7 @@
     scale = 1.0 / math.sqrt(HD)
 
     def kv(i, kh):
-        return (y + gray(3 - i)) % 4 * 2 + kh
+        return (y + gray(3 - i)) % 4 * 2 + (x // 2 + 1 + kh) % 2
 
     def columns_of(i, kh):
         return pl.ds(pl.multiple_of(kv(i, kh) * 128, 128), 128)
@@ -377,7 +394,8 @@
             gather_values(i, hb, cb)
             if cb == 1:
                 join(i, hb)
-                post(i, hb)
+        for hb in range(2):
+            post(i, hb)
     o_in[chip] = o_out[chip]
     st_in[chip] = st_out[chip]
     take(st_recv, st_in.at[pl.ds(0, 31)])
@@ -444,8 +462,9 @@
         take(s1_send, x_in.at[0, pl.ds(0, 96)])
 
     take(sq_send, sq_in.at[pl.ds(0, 15)])
-    take(x_send, x_in.at[pl.ds(0, 8)])
-    take(xf_send, x_in.at[pl.ds(0, 7)])
+    take(x_send, o_out.at[pl.ds(0, 24)])
+    take(xl_send, o_out.at[pl.ds(0, 15)])
+    take(xf_send, o_out.at[pl.ds(0, 21)])
     take(a_send, a_in.at[pl.ds(0, 15)])
     take(p_send, p_in.at[pl.ds(0, 15)])
     take(g_send, g_in.at[pl.ds(0, 31)])
@@ -505,7 +524,7 @@
             vmem((64, 16, 128), bf16),
             vmem((64, 16, 128), bf16),
             dma((4,)), dma((3,)), dma((3,)),
-            dma, dma((4,)), dma, dma, dma, dma((16,)), dma, dma, dma, dma,
+            dma, dma((4,)), dma, dma, dma, dma((16,)), dma, dma, dma, dma, dma, dma,
             dma, dma, dma, dma, dma, dma, dma, dma, dma, dma,
         ],
         compiler_params=pltpu.CompilerParams(

time: 53.3 us -> 52.8 us (level)
  no operation moved by 1% of the time
where the time goes in v5:
time: 52.8 us; the launch traced here: 52.7 us
  Pallas kernels  52.1 us (99%)
  other arithmetic  0.6 us (1%)
    pallas_call x1, Pallas kernels, shards(): pl.pallas_call(kernel, out_shape=pltpu.VMEM((rows, local_width), f32), in...  52.1 us

profile of v5, /device:TPU:1, one launch (start us, length us, event | category | flops | bytes accessed | tf_op | source)
XLA Modules:
  0.0 52.7 jit_solution(15130348663320946819)
XLA Ops:
  0.0 0.0 copy-start
  0.0 52.1 %layer.1 = f32[32,128]{1,0:T(8,128)S(1)} custom-call(bf16[32,128]{1,0:T(8,128)(2,1)} %bitcast.6, bf16[1,128]{1,0:T(2,128)(2,1)} %bitcast.7, f32[1,128]{1,0:T(1,128)} %constant.2.clone.freqs, s32[16]{0:T(128)} %lens.1, s32[16]{0:T(128)} %places.1, bf16[160,2048]{1,0:T(8,128)(2,1)} %bitcast.5, bf16[128,8192]{1,0:T(8,128)(2,1)} %wo_hbm.1, ...), custom_call_target="tpu_custom_call" | custom-call | tf_op jit(solution)/shard_map/layer/pallas_call | solution.py:488
  52.1 0.0 copy-done
  52.1 0.6 %add_convert_fusion = bf16[2,16,128]{2,1,0:T(8,128)(2,1)} fusion(f32[2,16,128]{2,1,0:T(8,128)S(1)} %bitcast.4, bf16[2,16,128]{2,1,0:T(8,128)(2,1)S(1)} %copy-done), kind=kLoop, calls=%fused_computation | loop fusion | flops 12288 | bytes 32768 | tf_op jit(solution)/shard_map/convert_element_type | solution.py:538
Async XLA Ops:
  0.0 52.1 %copy-start = (bf16[2,16,128]{2,1,0:T(8,128)(2,1)S(1)}, bf16[2,16,128]{2,1,0:T(8,128)(2,1)}, u32[]{:S(2)}) copy-start(bf16[2,16,128]{2,1,0:T(8,128)(2,1)} %param.9) | copy-start | bytes 24580

commit v6 on v5

--- a/solution.py
+++ b/solution.py
@@ -357,7 +357,7 @@
             for t in range(2):
                 at = bs * 16 + t * 8
                 tb = t * 8 + bs
-                o32[hb, pl.ds(tb, 8, stride=16), :] = summed[at : at + 8]
+                o32[2 * (i % 2) + hb, pl.ds(tb, 8, stride=16), :] = summed[at : at + 8]
                 stat = jnp.where(lane8 == tb, total[at : at + 8], stat)
                 stat = jnp.where(lane8 == 32 + tb, peak[at : at + 8], stat)
         stats[i, hb] = (stat, pltpu.roll(stat, 16, 1))
@@ -365,7 +365,7 @@
     def post(i, hb):
         for p in range(4):
             dest = kv(i, hb) * 4 + p
-            o_out[dest] = o32[hb, p * 32 : p * 32 + 32, :].astype(jnp.bfloat16)
+            o_out[dest] = o32[2 * (i % 2) + hb, p * 32 : p * 32 + 32, :].astype(jnp.bfloat16)
             stat, turned = stats[i, hb]
             st_out[dest] = stat[2 * p : 2 * p + 1] + turned[2 * p + 1 : 2 * p + 2]
         for p in range(4):
@@ -394,8 +394,11 @@
             gather_values(i, hb, cb)
             if cb == 1:
                 join(i, hb)
-        for hb in range(2):
-            post(i, hb)
+            if i > 0 and (hb, cb) == (0, 0):
+                post(i - 1, 0)
+                post(i - 1, 1)
+    post(3, 0)
+    post(3, 1)
     o_in[chip] = o_out[chip]
     st_in[chip] = st_out[chip]
     take(st_recv, st_in.at[pl.ds(0, 31)])
@@ -515,7 +518,7 @@
             vmem((2, 2, 128, 128), f32),
             vmem((2, 128, 128), f32),
             vmem((2, 128, 128), f32),
-            vmem((2, 128, 128), f32),
+            vmem((4, 128, 128), f32),
             vmem((32, 32, 128), bf16),
             vmem((32, 1, 128), f32),
             vmem((32, 32, 128), bf16),

time: 52.8 us -> 52.5 us (level)
  no operation moved by 1% of the time
where the time goes in v6:
time: 52.5 us; the launch traced here: 52.4 us
  Pallas kernels  51.7 us (98%)
  other arithmetic  0.6 us (1%)
    pallas_call x1, Pallas kernels, shards(): pl.pallas_call(kernel, out_shape=pltpu.VMEM((rows, local_width), f32), in...  51.7 us

profile of v6, /device:TPU:1, one launch (start us, length us, event | category | flops | bytes accessed | tf_op | source)
XLA Modules:
  0.0 52.4 jit_solution(8474373344090489276)
XLA Ops:
  0.0 0.0 copy-start
  0.0 51.7 %layer.1 = f32[32,128]{1,0:T(8,128)S(1)} custom-call(bf16[32,128]{1,0:T(8,128)(2,1)} %bitcast.6, bf16[1,128]{1,0:T(2,128)(2,1)} %bitcast.7, f32[1,128]{1,0:T(1,128)} %constant.2.clone.freqs, s32[16]{0:T(128)} %lens.1, s32[16]{0:T(128)} %places.1, bf16[160,2048]{1,0:T(8,128)(2,1)} %bitcast.5, bf16[128,8192]{1,0:T(8,128)(2,1)} %wo_hbm.1, ...), custom_call_target="tpu_custom_call" | custom-call | tf_op jit(solution)/shard_map/layer/pallas_call | solution.py:491
  51.8 0.0 copy-done
  51.8 0.6 %add_convert_fusion = bf16[2,16,128]{2,1,0:T(8,128)(2,1)} fusion(f32[2,16,128]{2,1,0:T(8,128)S(1)} %bitcast.4, bf16[2,16,128]{2,1,0:T(8,128)(2,1)S(1)} %copy-done), kind=kLoop, calls=%fused_computation | loop fusion | flops 12288 | bytes 32768 | tf_op jit(solution)/shard_map/convert_element_type | solution.py:541
Async XLA Ops:
  0.0 51.8 %copy-start = (bf16[2,16,128]{2,1,0:T(8,128)(2,1)S(1)}, bf16[2,16,128]{2,1,0:T(8,128)(2,1)}, u32[]{:S(2)}) copy-start(bf16[2,16,128]{2,1,0:T(8,128)(2,1)} %param.9) | copy-start | bytes 24580
